TPU v7x, 32 devices: a whole 2x2x4 slice. The times are simulated.
32 devices in a mesh: blk: 16 (over z, y, core), col: 2 (over x).
Axes of the slice: x: 2, y: 2, z: 4, core: 2. Of those that a mesh axis runs over, the one named last changes fastest.
Arguments:
- counts: float32 [8192, 8192], P('blk', 'col'), may hold values from 0.1 to 10
- merge_map: int32 [8192, 1], replicated, may hold values from 0 to 4095, as said below
Outputs:
- merged: float32 [4096, 4096], P('blk', 'col')
- block_terms: float32 [4096], P('blk')
Inputs may be any that keep to these rules, and one draw needn't show every extreme that they name: `merge_map`: every new block is the image of exactly two old blocks. Let the owner of new block r be r // 256. The 512 old blocks i with i // 512 = s, for each s, map to new blocks of exactly 8 distinct owners, exactly 64 old blocks to each of them, and each owner receives from exactly 8 such s.
All inputs are finite; a program needn't handle non-finite values.
Results may differ from a plain program's by a relative error of at most 0.0003.
Values sent between devices are 32-bit elements; how exact they have to be, the bound alone decides.
No kernel may reach another device: no remote copies, remote signals or barrier semaphores. Data moves between devices by JAX's collectives and lax.ppermute only.
A program may use at most 128 MiB of HBM per device.

v0:
```python
import jax
import jax.numpy as jnp
from jax import lax
from jax.sharding import PartitionSpec as P

NB = 4096


HIGH = lax.Precision.HIGHEST


def one_hot_block(labels, count):
    targets = jnp.arange(count, dtype=jnp.int32)
    return (labels[:, None] == targets[None, :]).astype(jnp.float32)


def pack_rows(matrix, labels, owned, groups, capacity):
    width = matrix.shape[1]
    owner = labels // owned
    table = (owner[:, None] == jnp.arange(groups, dtype=jnp.int32)[None, :]).astype(jnp.int32)
    ranks = jnp.sum(jnp.cumsum(table, axis=0) * table, axis=1) - 1
    target = owner * capacity + ranks
    buffer = jnp.zeros((groups * capacity, width), jnp.float32).at[target].set(matrix)
    tags = jnp.full((groups * capacity,), -1, jnp.int32).at[target].set(labels)
    return (buffer.reshape(groups, capacity, width), tags.reshape(groups, capacity))


def unpack_rows(buffer, tags, owned):
    width = buffer.shape[2]
    local_ids = tags.reshape(-1) - lax.axis_index("blk") * owned
    table = one_hot_block(local_ids, owned)
    flat = buffer.reshape(-1, width)
    return lax.dot_general(
        table, flat, (((0,), (0,)), ((), ())), precision=HIGH, preferred_element_type=jnp.float32
    )


def shards(counts, merge_map):
    row_len = counts.shape[0]
    col_len = counts.shape[1]
    groups = lax.axis_size("blk")
    columns_axis = lax.axis_size("col")
    owned = NB // groups
    owned_cols = NB // columns_axis
    fanout = min(groups // 2, row_len // 2)
    capacity = row_len // fanout
    ids = merge_map[:, 0]
    row_labels = lax.dynamic_slice_in_dim(ids, lax.axis_index("blk") * row_len, row_len, 0)
    col_labels = lax.dynamic_slice_in_dim(ids, lax.axis_index("col") * col_len, col_len, 0)
    buffer, tags = pack_rows(counts, row_labels, owned, groups, capacity)
    got_rows, got_tags = (
        lax.all_to_all(buffer, "blk", split_axis=0, concat_axis=0, tiled=True),
        lax.all_to_all(tags, "blk", split_axis=0, concat_axis=0, tiled=True),
    )
    row_merged = unpack_rows(got_rows, got_tags, owned)
    table = one_hot_block(col_labels, owned_cols * lax.axis_size("col"))
    merged = lax.psum_scatter(
        lax.dot_general(
            table,
            row_merged,
            (((0,), (1,)), ((), ())),
            precision=HIGH,
            preferred_element_type=jnp.float32,
        ),
        "col",
        scatter_dimension=0,
        tiled=True,
    ).T
    in_total = lax.psum(jnp.sum(merged, axis=0), "blk")
    out_total, total = lax.psum((jnp.sum(merged, axis=1), jnp.sum(in_total)), "col")
    share = merged / out_total[:, None]
    ratio = merged * total / (out_total[:, None] * in_total[None, :])
    partial_terms = jnp.sum(share * jnp.log(ratio), axis=1)
    block_terms = lax.psum(partial_terms, "col")
    return (merged, block_terms)


def solution(mesh):
    placed = (P("blk", "col"), P())
    return jax.shard_map(
        shards, mesh=mesh, in_specs=placed, out_specs=(P("blk", "col"), P("blk")), check_vma=False
    )
```

profile of v0, /device:TPU:0, one launch (start us, length us, event | category | flops | bytes accessed | tf_op | source)
XLA Modules:
  0.0 571.0 jit_solution(2469705221501328612)
XLA Ops:
  7.2 0.7 and_select_fusion
  7.9 1.2 reduce-window.6
  9.0 0.2 slice_reduce_fusion
  9.3 0.1 fusion.9
  9.4 2.4 scatter_custom_fusion
  11.9 0.7 all_to_all.9
  12.6 7.4 %all-to-all-start = ((s32[16,1,64]{2,1,0:T(1,128)}), s32[16,1,64]{2,1,0:T(1,128)S(1)}, u32[]{:S(2)}, u32[]{:S(2)}) async-start(s32[16,1,64]{2,1,0:T(1,128)} %all_to_all.9), calls=%async_computation | async-start | bytes 16384 | tf_op jit(solution)/shard_map/all_to_all | solution.py:53
  20.0 14.8 %scatter_custom_fusion.1 = f32[1024,4096]{1,0:T(8,128)} fusion(s32[512]{0:T(512)S(1)} %bitcast.34, f32[512,4096]{1,0:T(8,128)} %param.2, f32[]{:T(128)} %constant.48.clone.1), kind=kCustom, calls=%fused_computation.6 | custom fusion | bytes 16777728 | tf_op jit(solution)/shard_map/scatter | solution.py:23
  34.7 0.0 all-to-all-done
  34.8 0.0 copy-start
  34.8 6.2 %all-to-all-start.1 = ((f32[16,64,4096]{2,1,0:T(8,128)}), f32[16,64,4096]{2,1,0:T(8,128)}, u32[]{:S(2)}, u32[]{:S(2)}) async-start(f32[16,64,4096]{2,1,0:T(8,128)} %bitcast.27), calls=%async_computation.1 | async-start | bytes 33554432 | tf_op jit(solution)/shard_map/all_to_all | solution.py:52
  41.0 0.2 reduce-scatter.2.cloned.1.call-start
  41.2 0.0 copy-done
  41.3 0.1 sub.30
  41.3 296.3 %all-to-all-done.1 = f32[16,64,4096]{2,1,0:T(8,128)} async-done(((f32[16,64,4096]{2,1,0:T(8,128)}), f32[16,64,4096]{2,1,0:T(8,128)}, u32[]{:S(2)}, u32[]{:S(2)}) %all-to-all-start.1) | async-done | bytes 16777248 | tf_op jit(solution)/shard_map/all_to_all | solution.py:52
  337.6 12.5 %fusion.6 = f32[256,4096]{1,0:T(8,128)S(1)} fusion(f32[1024,4096]{1,0:T(8,128)} %bitcast.8, s32[1024]{0:T(1024)S(1)} %sub.30), kind=kOutput, calls=%fused_computation.10 | convolution fusion | flops 12885164032 | bytes 20975616 | tf_op jit(solution)/shard_map/dot_general | solution.py:33
  350.1 41.0 %fusion.1 = f32[4096,256]{1,0:T(8,128)} fusion(f32[256,4096]{1,0:T(8,128)S(1)} %fusion.6, s32[4096]{0:T(1024)S(1)} %bitcast.31), kind=kOutput, calls=%fused_computation.4 | convolution fusion | flops 51573161984 | bytes 8404992 | tf_op jit(solution)/shard_map/dot_general | solution.py:58
  391.1 0.0 reduce-scatter.2.cloned.1.call-update
  391.1 120.1 %reduce-scatter.2.cloned.1.call-done = f32[2048,256]{1,0:T(8,128)} async-done(((f32[4096,256]{1,0:T(8,128)}), f32[2048,256]{1,0:T(8,128)}) %reduce-scatter.2.cloned.1.call-update) | async-done | bytes 2097168 | tf_op jit(solution)/shard_map/reduce_scatter | solution.py:57
  511.2 1.9 fusion.13
  513.1 33.5 %psum.29 = f32[2048]{0:T(1024)S(1)} all-reduce(f32[2048]{0:T(1024)S(1)} %get-tuple-element.7), channel_id=1, replica_groups=mesh['blk'=16,'col'=2] {'blk'}, use_global_device_ids=true, to_apply=%region_9.10 | all-reduce | flops 2048 | bytes 16384 | tf_op jit(solution)/shard_map/psum | solution.py:69
  546.7 0.6 reduce_sum.48
  547.3 5.5 all-reduce
  552.8 2.9 multiply_reduce_fusion
  555.7 5.5 psum.31
  561.2 2.9 copy.6
  (7 shorter events, 0.1 us)
Async XLA Ops:
  12.6 22.2 %all-to-all-start = ((s32[16,1,64]{2,1,0:T(1,128)}), s32[16,1,64]{2,1,0:T(1,128)S(1)}, u32[]{:S(2)}, u32[]{:S(2)}) async-start(s32[16,1,64]{2,1,0:T(1,128)} %all_to_all.9), calls=%async_computation | async-start | bytes 16384 | tf_op jit(solution)/shard_map/all_to_all | solution.py:53
  34.8 6.4 %copy-start = (s32[8192,1]{0,1:T(1,128)S(1)}, s32[8192,1]{0,1:T(1,128)}, u32[]{:S(2)}) copy-start(s32[8192,1]{0,1:T(1,128)} %param.3) | copy-start | bytes 98308
  34.8 302.8 %all-to-all-start.1 = ((f32[16,64,4096]{2,1,0:T(8,128)}), f32[16,64,4096]{2,1,0:T(8,128)}, u32[]{:S(2)}, u32[]{:S(2)}) async-start(f32[16,64,4096]{2,1,0:T(8,128)} %bitcast.27), calls=%async_computation.1 | async-start | bytes 33554432 | tf_op jit(solution)/shard_map/all_to_all | solution.py:52
  41.0 470.2 %reduce-scatter.2.cloned.1.call-start = ((), (), s32[]{:S(2)}) async-start(), calls=%async_computation.3 | async-start | bytes 6291456 | tf_op jit(solution)/shard_map/reduce_scatter | solution.py:57
Sparse Core Ops, SparseCore 0:
  391.2 119.9 reduce-scatter.1
where the time goes:
time: 571 us
  waiting for transfers between devices  416 us (73%)
  matrix products  53.5 us (9%)
  blocking collectives  44.6 us (8%)
  local copies, waits for them, and re-layouts  21.1 us (4%)
  between operations  14.1 us (2%)
  starting transfers between devices  13.8 us (2%)
  other arithmetic  7.52 us (1%)
    all_to_all x1, waiting for transfers between devices, shards(): lax.all_to_all(buffer, 'blk', split_axis=0, concat_axis=0, tiled=True)  296 us
    reduce_scatter x1, waiting for transfers between devices, shards(): lax.psum_scatter(lax.dot_general(table, row_merged, (((0,), (1,)), ((), (...  120 us
    dot_general x1, matrix products, shards(): lax.dot_general(table, row_merged, (((0,), (1,)), ((), ())), precision=HI...  41 us
    psum x1, blocking collectives, shards(): in_total = lax.psum(jnp.sum(merged, axis=0), 'blk')  33.5 us
    scatter x1, local copies, waits for them, and re-layouts, pack_rows(): jnp.zeros((groups * capacity, width), jnp.float32).at[target].set(matrix)  14.8 us
    dot_general x1, matrix products, unpack_rows(): lax.dot_general(table, flat, (((0,), (0,)), ((), ())), precision=HIGH, pr...  12.5 us
  transfers between devices with their start and end apart: 3, of which 2 were waited for; matrix products, arithmetic and copies ran while one was open for 3% of the time, Pallas kernels for 0%

commit v1 on v0

v1 whole, which is shorter than its diff:
```python
import functools

import jax
import jax.numpy as jnp
from jax import lax
from jax.experimental import pallas as pl
from jax.experimental.pallas import tpu as pltpu
from jax.sharding import PartitionSpec as P

PARTS = (2, 4, 4, 4, 2)
F32, BF16, I32 = jnp.float32, jnp.bfloat16, jnp.int32


def widths(owned_cols):
    unit = owned_cols // sum(PARTS)
    return [p * unit for p in PARTS] if unit % 128 == 0 else [owned_cols]


def split(x):
    hi = x.astype(BF16)
    return hi, (x - hi.astype(F32)).astype(BF16)


def hot(labels, count, base=0):
    index = lax.broadcasted_iota(I32, (count, labels.shape[1]), 0) + base
    return jnp.where(index == labels, 1.0, 0.0).astype(BF16)


def mxu(a, b, dims):
    return lax.dot_general(a, b, (dims, ((), ())), preferred_element_type=F32)


def call(kernel, flops, nbytes, **kw):
    return pl.pallas_call(
        kernel, cost_estimate=pl.CostEstimate(flops=flops, bytes_accessed=nbytes, transcendentals=0), **kw
    )


def columns_kernel(start, owned, present_ref, pos_ref, counts_ref, *out_refs):
    rows, width = out_refs[0].shape
    k = pl.program_id(0)
    per_column = present_ref.shape[1] // len(out_refs)

    @pl.when(k == 0)
    def _():
        for out_ref in out_refs:
            out_ref[...] = jnp.zeros_like(out_ref)

    hi, lo = split(counts_ref[...])
    both = jnp.concatenate([hi, lo], axis=0)
    for c, out_ref in enumerate(out_refs):
        for b in range(width // owned):
            block = c * per_column + start // owned + b

            @pl.when(present_ref[k, block] > 0)
            def _():
                part = mxu(both, hot(pos_ref[...], owned, block * owned), ((1,), (1,)))
                out_ref[:, b * owned : (b + 1) * owned] += part[:rows] + part[rows:]


def merge_columns(counts, pos, present, owned, columns, start, width):
    rows, cols = counts.shape
    tile = cols // present.shape[0]
    return call(
        functools.partial(columns_kernel, start, owned),
        2 * rows * cols * columns * width, 4 * rows * (cols + columns * width),
        grid_spec=pltpu.PrefetchScalarGridSpec(
            num_scalar_prefetch=1,
            grid=(cols // tile,),
            in_specs=[pl.BlockSpec((1, tile), lambda k, _: (0, k)), pl.BlockSpec((rows, tile), lambda k, _: (0, k))],
            out_specs=[pl.BlockSpec((rows, width), lambda k, _: (0, 0))] * columns,
        ),
        out_shape=[jax.ShapeDtypeStruct((rows, width), F32)] * columns,
    )(present, pos, counts)


def slots_kernel(pos_ref, *refs):
    ins, out_ref, sum_ref, table = refs[:-3], refs[-3], refs[-2], refs[-1]

    @pl.when(pl.program_id(0) == 0)
    def _():
        table[...] = hot(pos_ref[...], table.shape[0])

    total = ins[0][...]
    for ref in ins[1:]:
        total += ref[...]
    sum_ref[...] = jnp.sum(total, axis=0, keepdims=True)
    hi, lo = split(total)
    out_ref[...] = mxu(table[...], hi, ((1,), (0,))) + mxu(table[...], lo, ((1,), (0,)))


def fill_slots(pos, ins, slots):
    rows, width = ins[0].shape
    tile = min(width, 256)
    return call(
        slots_kernel, 4 * slots * rows * width, 4 * width * (rows * len(ins) + slots),
        grid=(width // tile,),
        in_specs=[pl.BlockSpec((1, rows), lambda k: (0, 0))] + [pl.BlockSpec((rows, tile), lambda k: (0, k))] * len(ins),
        out_specs=[pl.BlockSpec((slots, tile), lambda k: (0, k)), pl.BlockSpec((1, tile), lambda k: (0, k))],
        out_shape=[jax.ShapeDtypeStruct((slots, width), F32), jax.ShapeDtypeStruct((1, width), F32)],
        scratch_shapes=[pltpu.VMEM((slots, rows), BF16)],
    )(pos, *ins)


def rows_kernel(pos_ref, got_ref, keep_ref, send_ref):
    peers, _, cap, tile = got_ref.shape
    for side, ref in enumerate((keep_ref, send_ref)):
        hi, lo = split(got_ref[:, side].reshape(peers * cap, tile))
        table = hot(pos_ref[side : side + 1, :], ref.shape[0])
        ref[...] = mxu(table, hi, ((1,), (0,))) + mxu(table, lo, ((1,), (0,)))


def merge_rows(pos, got, owned):
    peers, _, cap, width = got.shape
    tile = min(width, 256)
    return call(
        rows_kernel, 8 * owned * peers * cap * width, 4 * width * (2 * owned + 2 * peers * cap),
        grid=(width // tile,),
        in_specs=[
            pl.BlockSpec((2, peers * cap), lambda k: (0, 0)),
            pl.BlockSpec((peers, 2, cap, tile), lambda k: (0, 0, 0, k)),
        ],
        out_specs=[pl.BlockSpec((owned, tile), lambda k: (0, k))] * 2,
        out_shape=[jax.ShapeDtypeStruct((owned, width), F32)] * 2,
    )(pos, got)


def fold(x):
    return sum(x[:, j : j + 128] for j in range(0, x.shape[1], 128))


def terms(block, in_total, new):
    return fold(block * jnp.log(block * (new / in_total))), fold(block)


def early_kernel(plan, new, in_total_ref, *refs):
    n = len(plan)
    keeps, others, (merged_ref, logs_ref, out_ref) = refs[:n], refs[n : 2 * n], refs[2 * n :]
    start, logs, out = 0, 0.0, 0.0
    for keep, other, width in zip(keeps, others, plan):
        block = keep[...] + other[...]
        merged_ref[:, start : start + width] = block
        more = terms(block, in_total_ref[:, start : start + width], new)
        logs, out, start = logs + more[0], out + more[1], start + width
    logs_ref[...], out_ref[...] = logs, out


def finish_early(plan, new, in_total, keeps, others):
    owned, total = keeps[0].shape[0], sum(plan)
    n, done = len(plan) - 1, sum(plan[:-1])
    tile = min(owned, 64)
    blocks = [pl.BlockSpec((tile, w), lambda k: (k, 0)) for w in plan[:-1]]
    lanes = pl.BlockSpec((tile, 128), lambda k: (k, 0))
    return call(
        functools.partial(early_kernel, plan[:-1], new), 20 * owned * done, 12 * owned * done,
        grid=(owned // tile,),
        in_specs=[pl.BlockSpec((1, total), lambda k: (0, 0))] + blocks * 2,
        out_specs=[pl.BlockSpec((tile, done), lambda k: (k, 0)), lanes, lanes],
        out_shape=[jax.ShapeDtypeStruct((owned, total), F32)] + [jax.ShapeDtypeStruct((owned, 128), F32)] * 2,
    )(in_total, *keeps[:n], *others[:n])


def last_kernel(new, in_total_ref, keep_ref, other_ref, *refs):
    merged_ref, part_ref = refs[-2:]
    width = keep_ref.shape[1]
    block = keep_ref[...] + other_ref[...]
    merged_ref[...] = block
    logs, out = terms(block, in_total_ref[:, in_total_ref.shape[1] - width :], new)
    if len(refs) > 2:
        logs, out = logs + refs[1][...], out + refs[2][...]
    row = lax.broadcasted_iota(I32, part_ref.shape, 0)
    logs = jnp.sum(logs.T, axis=0, keepdims=True)
    out = jnp.sum(out.T, axis=0, keepdims=True)
    total = jnp.sum(in_total_ref[...], axis=1, keepdims=True)
    part_ref[...] = jnp.where(row == 0, logs, jnp.where(row == 1, out, total))


def finish_last(plan, new, in_total, keep, other, early):
    owned, width, total = keep.shape[0], plan[-1], sum(plan)
    at = (total - width) // width
    whole = pl.BlockSpec((owned, width), lambda k: (0, 0))
    lanes = [pl.BlockSpec((owned, 128), lambda k: (0, 0))] * 2
    return call(
        functools.partial(last_kernel, new), 20 * owned * width, 12 * owned * width,
        grid=(1,),
        in_specs=[pl.BlockSpec((1, total), lambda k: (0, 0)), whole, whole]
        + ([pl.BlockSpec(memory_space=pl.ANY)] + lanes if early else []),
        out_specs=[pl.BlockSpec((owned, width), lambda k: (0, at)), pl.BlockSpec((8, owned), lambda k: (0, 0))],
        out_shape=[jax.ShapeDtypeStruct((owned, total), F32), jax.ShapeDtypeStruct((8, owned), F32)],
        input_output_aliases={3: 0} if early else {},
    )(in_total, keep, other, *early)


def tags_of(ids, mine, capacity):
    rank = jnp.cumsum(mine.astype(I32), axis=1) - 1
    hit = mine[:, None, :] & (rank[:, None, :] == jnp.arange(capacity, dtype=I32)[None, :, None])
    return jnp.max(jnp.where(hit, ids[:, None, :], -1), axis=2)


def body(counts, merge_map):
    rows, cols = counts.shape
    groups, columns = lax.axis_size("blk"), lax.axis_size("col")
    blk, col = lax.axis_index("blk"), lax.axis_index("col")
    ids = merge_map[:, 0]
    new = ids.shape[0] // 2
    owned, owned_cols = new // groups, new // columns
    fanout = min(groups // 2, rows // 2)
    cap = rows // fanout
    half = groups // 2
    plan = widths(owned_cols)
    starts = [sum(plan[:q]) for q in range(len(plan))]
    row_labels = lax.dynamic_slice_in_dim(ids, blk * rows, rows, 0)
    col_labels = lax.dynamic_slice_in_dim(ids, col * cols, cols, 0)

    step_of = lax.rem(col_labels // owned_cols - col + columns, columns)
    col_pos = step_of * owned_cols + lax.rem(col_labels, owned_cols)
    mapped = (col_pos // owned).reshape(cols // rows, rows, 1) == jnp.arange(groups, dtype=I32)
    present = jnp.max(mapped.astype(I32), axis=1)

    owner = row_labels // owned
    table = (owner[:, None] == jnp.arange(groups, dtype=I32)[None, :]).astype(I32)
    rank = jnp.sum(jnp.cumsum(table, axis=0) * table, axis=1) - 1
    place = lax.rem(owner, half) * 2 + (owner // half != blk // half).astype(I32)
    row_pos = (place * cap + rank)[None, :]

    base = (blk // half) * half
    peers = lax.dynamic_slice_in_dim(ids.reshape(groups, rows), base, half, 0)
    take_pos = []
    for agg in (blk, lax.rem(blk + half, groups)):
        tags = tags_of(peers, peers // owned == agg, cap).reshape(-1)
        take_pos.append(jnp.where(tags < 0, -1, tags - agg * owned))
    take_pos = jnp.stack(take_pos)

    sums, keeps, others = [], [], []
    for q, width in enumerate(plan):
        parts = list(merge_columns(counts, col_pos[None, :], present, owned, columns, starts[q], width))
        for step in range(1, columns):
            parts[step] = lax.ppermute(parts[step], "col", [(i, (i + step) % columns) for i in range(columns)])
        slotted, column_sum = fill_slots(row_pos, parts, groups * cap)
        sums.append(column_sum)
        got = lax.all_to_all(
            slotted.reshape(half, 2, cap, width), "blk", split_axis=0, concat_axis=0, tiled=True,
            axis_index_groups=[list(range(half)), list(range(half, groups))],
        )
        keep, send = merge_rows(take_pos, got, owned)
        others.append(lax.ppermute(send, "blk", [(i, (i + half) % groups) for i in range(groups)]))
        keeps.append(keep)
    sums = jnp.broadcast_to(jnp.concatenate(sums, axis=1), (groups, owned_cols))
    sums = lax.all_to_all(sums, "blk", split_axis=0, concat_axis=0, tiled=True)
    in_total = jnp.sum(sums, axis=0, keepdims=True)
    early = ()
    if len(plan) > 1:
        early = finish_early(plan, new, in_total, keeps, others)
    merged, part = finish_last(plan, new, in_total, keeps[-1], others[-1], early)
    if columns == 2:
        part += lax.ppermute(part, "col", [(0, 1), (1, 0)])
    else:
        part = lax.psum(part, "col")
    block_terms = part[0] / part[1] + jnp.log(part[2] / (part[1] * new))
    return (merged, block_terms)


def solution(mesh):
    placed = (P("blk", "col"), P())
    return jax.shard_map(body, mesh=mesh, in_specs=placed, out_specs=(P("blk", "col"), P("blk")), check_vma=False)
```

time: 571 us -> 339 us (0.59)
  waiting for transfers between devices: 416 us -> 98 us
  Pallas kernels: 0 us -> 101 us
  matrix products: 53.5 us -> 0 us
  blocking collectives: 44.6 us -> 76.5 us
  starting transfers between devices: 13.8 us -> 38.1 us
  between operations: 14.1 us -> 0.88 us
  local copies, waits for them, and re-layouts: 21.1 us -> 12.1 us
    all_to_all x2 -> x5, waiting for transfers between devices: 296 us -> 0.01 us  [body(): lax.all_to_all(slotted.reshape(half, 2, cap, width), 'blk', split_axis=0,...]
    reduce_scatter x1 -> x0, waiting for transfers between devices: 120 us -> none  [shards(): lax.psum_scatter(lax.dot_general(table, row_merged, (((0,), (1,)), ((), (...]
    pallas_call x0 -> x17, Pallas kernels: none -> 101 us  [the longest x5 62.9 us: merge_columns(): call(functools.partial(columns_kernel, start, owned), 2 * rows * cols * c...]
    ppermute x0 -> x11, waiting for transfers between devices: none -> 98 us  [the longest x5 94.9 us: body(): lax.ppermute(parts[step], 'col', [(i, (i + step) % columns) for i in rang...]
    all_to_all x0 -> x1, blocking collectives: none -> 76.5 us  [body(): sums = lax.all_to_all(sums, 'blk', split_axis=0, concat_axis=0, tiled=True)]
    dot_general x2 -> x0, matrix products: 53.5 us -> none  [the longest x1 41 us: shards(): lax.dot_general(table, row_merged, (((0,), (1,)), ((), ())), precision=HI...]
    psum x3 -> x0, blocking collectives: 44.6 us -> none  [the longest x1 33.5 us: shards(): in_total = lax.psum(jnp.sum(merged, axis=0), 'blk')]
    ppermute x0 -> x11, starting transfers between devices: none -> 17.6 us  [the longest x5 8.49 us: body(): lax.ppermute(send, 'blk', [(i, (i + half) % groups) for i in range(groups)])]
  transfers between devices with their start and end apart: 3 -> 16, of which waited for: 2 -> 6; matrix products, arithmetic and copies ran while one was open for 3% -> 3% of each run, Pallas kernels for 0% -> 25%
where the time goes in v1:
time: 339 us; the launch traced here: 337 us
  Pallas kernels  101 us (30%)
  waiting for transfers between devices  98 us (29%)
  blocking collectives  76.5 us (23%)
  starting transfers between devices  38.1 us (11%)
  local copies, waits for them, and re-layouts  12.1 us (4%)
  other arithmetic  10.7 us (3%)
    ppermute x5, waiting for transfers between devices, body(): lax.ppermute(parts[step], 'col', [(i, (i + step) % columns) for i in rang...  94.9 us
    all_to_all x1, blocking collectives, body(): sums = lax.all_to_all(sums, 'blk', split_axis=0, concat_axis=0, tiled=True)  76.5 us
    pallas_call x5, Pallas kernels, merge_columns(): call(functools.partial(columns_kernel, start, owned), 2 * rows * cols * c...  62.9 us
    all_to_all x5, starting transfers between devices, body(): lax.all_to_all(slotted.reshape(half, 2, cap, width), 'blk', split_axis=0,...  20.4 us
    pallas_call x5, Pallas kernels, fill_slots(): call(slots_kernel, 4 * slots * rows * width, 4 * width * (rows * len(ins)...  17.4 us
    pallas_call x5, Pallas kernels, merge_rows(): call(rows_kernel, 8 * owned * peers * cap * width, 4 * width * (2 * owned...  14.5 us
    unnamed x45, local copies, waits for them, and re-layouts  10.4 us
    ppermute x5, starting transfers between devices, body(): lax.ppermute(send, 'blk', [(i, (i + half) % groups) for i in range(groups)])  8.49 us
  transfers between devices with their start and end apart: 16, of which 6 were waited for; matrix products, arithmetic and copies ran while one was open for 3% of the time, Pallas kernels for 25%

profile of v1, /device:TPU:0, one launch (start us, length us, event | category | flops | bytes accessed | tf_op | source)
XLA Modules:
  0.0 337.2 jit_solution(7252427713478369013)
XLA Ops:
  0.6 1.4 fusion.14.pos_ref
  2.9 0.8 convert_reduce_fusion.present_ref
  3.7 11.3 %shard_map.49 = (f32[512,256]{1,0:T(8,128)}, f32[512,256]{1,0:T(8,128)}) custom-call(s32[8,16]{1,0:T(8,128)} %convert_reduce_fusion.present_ref, s32[1,4096]{1,0:T(1,128)} %fusion.14.pos_ref, f32[512,4096]{1,0:T(8,128)} %counts_ref.9), custom_call_target="tpu_custom_call" | custom-call | flops 2147483648 | bytes 9437184 | tf_op jit(solution)/shard_map/pallas_call | solution.py:64
  15.0 1.5 collective-permute-start.4
  16.6 1.2 reduce-window.20
  18.7 10.8 %collective-permute-done.4.refs_1_ = f32[512,256]{1,0:T(8,128)S(1)} collective-permute-done((f32[512,256]{1,0:T(8,128)}, f32[512,256]{1,0:T(8,128)S(1)}, u32[]{:S(2)}, u32[]{:S(2)}) %collective-permute-start.4) | collective-permute-done | bytes 524320 | tf_op jit(solution)/shard_map/ppermute | solution.py:238
  29.6 0.8 copy-done.18
  30.4 2.9 shard_map.50
  33.3 4.6 %all-to-all-start.1 = ((f32[8,2,64,256]{3,2,1,0:T(8,128)}), f32[8,2,64,256]{3,2,1,0:T(8,128)S(1)}, u32[]{:S(2)}, u32[]{:S(2)}) async-start(f32[8,2,64,256]{3,2,1,0:T(8,128)} %bitcast.62), calls=%async_computation.1 | async-start | bytes 2097152 | tf_op jit(solution)/shard_map/all_to_all | solution.py:241
  37.9 14.0 %shard_map.47 = (f32[512,512]{1,0:T(8,128)}, f32[512,512]{1,0:T(8,128)}) custom-call(s32[8,16]{1,0:T(8,128)} %convert_reduce_fusion.present_ref, s32[1,4096]{1,0:T(1,128)} %fusion.14.pos_ref, f32[512,4096]{1,0:T(8,128)} %counts_ref.9), custom_call_target="tpu_custom_call" | custom-call | flops 4294967296 | bytes 10485760 | tf_op jit(solution)/shard_map/pallas_call | solution.py:64
  52.7 25.0 %collective-permute-done.3.refs_1_ = f32[512,512]{1,0:T(8,128)S(1)} collective-permute-done((f32[512,512]{1,0:T(8,128)}, f32[512,512]{1,0:T(8,128)S(1)}, u32[]{:S(2)}, u32[]{:S(2)}) %collective-permute-start.3) | collective-permute-done | bytes 1048608 | tf_op jit(solution)/shard_map/ppermute | solution.py:238
  77.7 1.0 copy-done.15
  78.7 3.8 %shard_map.48 = (f32[1024,512]{1,0:T(8,128)}, f32[1,512]{1,0:T(1,128)}) custom-call(s32[1,512]{1,0:T(1,128)} %fusion.21.pos_ref, f32[512,512]{1,0:T(8,128)} %get-tuple-element.46.refs_0_, f32[512,512]{1,0:T(8,128)} %copy-done.15), custom_call_target="tpu_custom_call" | custom-call | flops 1073741824 | bytes 4194304 | tf_op jit(solution)/shard_map/pallas_call | solution.py:95
  82.5 1.0 copy-done.2
  83.5 3.8 %all-to-all-start.5 = ((f32[8,2,64,512]{3,2,1,0:T(8,128)}), f32[8,2,64,512]{3,2,1,0:T(8,128)S(1)}, u32[]{:S(2)}, u32[]{:S(2)}) async-start(f32[8,2,64,512]{3,2,1,0:T(8,128)} %bitcast.59), calls=%async_computation.5 | async-start | bytes 4194304 | tf_op jit(solution)/shard_map/all_to_all | solution.py:241
  87.3 13.1 %shard_map.45 = (f32[512,512]{1,0:T(8,128)}, f32[512,512]{1,0:T(8,128)}) custom-call(s32[8,16]{1,0:T(8,128)} %convert_reduce_fusion.present_ref, s32[1,4096]{1,0:T(1,128)} %fusion.14.pos_ref, f32[512,4096]{1,0:T(8,128)} %counts_ref.9), custom_call_target="tpu_custom_call" | custom-call | flops 4294967296 | bytes 10485760 | tf_op jit(solution)/shard_map/pallas_call | solution.py:64
  100.4 2.2 collective-permute-start.2
  102.6 24.1 %collective-permute-done.2.refs_1_ = f32[512,512]{1,0:T(8,128)S(1)} collective-permute-done((f32[512,512]{1,0:T(8,128)}, f32[512,512]{1,0:T(8,128)S(1)}, u32[]{:S(2)}, u32[]{:S(2)}) %collective-permute-start.2) | collective-permute-done | bytes 1048608 | tf_op jit(solution)/shard_map/ppermute | solution.py:238
  126.7 1.0 copy-done.16
  127.7 3.9 %shard_map.46 = (f32[1024,512]{1,0:T(8,128)}, f32[1,512]{1,0:T(1,128)}) custom-call(s32[1,512]{1,0:T(1,128)} %fusion.21.pos_ref, f32[512,512]{1,0:T(8,128)} %get-tuple-element.43.refs_0_, f32[512,512]{1,0:T(8,128)} %copy-done.16), custom_call_target="tpu_custom_call" | custom-call | flops 1073741824 | bytes 4194304 | tf_op jit(solution)/shard_map/pallas_call | solution.py:95
  131.6 1.3 copy-done
  132.9 4.4 %all-to-all-start.4 = ((f32[8,2,64,512]{3,2,1,0:T(8,128)}), f32[8,2,64,512]{3,2,1,0:T(8,128)}, u32[]{:S(2)}, u32[]{:S(2)}) async-start(f32[8,2,64,512]{3,2,1,0:T(8,128)} %bitcast.60), calls=%async_computation.4 | async-start | bytes 4194304 | tf_op jit(solution)/shard_map/all_to_all | solution.py:241
  137.3 13.0 %shard_map.43 = (f32[512,512]{1,0:T(8,128)}, f32[512,512]{1,0:T(8,128)}) custom-call(s32[8,16]{1,0:T(8,128)} %convert_reduce_fusion.present_ref, s32[1,4096]{1,0:T(1,128)} %fusion.14.pos_ref, f32[512,4096]{1,0:T(8,128)} %counts_ref.9), custom_call_target="tpu_custom_call" | custom-call | flops 4294967296 | bytes 10485760 | tf_op jit(solution)/shard_map/pallas_call | solution.py:64
  150.3 3.1 collective-permute-start.1
  153.5 23.9 %collective-permute-done.1.refs_1_ = f32[512,512]{1,0:T(8,128)S(1)} collective-permute-done((f32[512,512]{1,0:T(8,128)}, f32[512,512]{1,0:T(8,128)S(1)}, u32[]{:S(2)}, u32[]{:S(2)}) %collective-permute-start.1) | collective-permute-done | bytes 1048608 | tf_op jit(solution)/shard_map/ppermute | solution.py:238
  177.4 1.1 copy-done.17
  178.5 3.8 %shard_map.44 = (f32[1024,512]{1,0:T(8,128)}, f32[1,512]{1,0:T(1,128)}) custom-call(s32[1,512]{1,0:T(1,128)} %fusion.21.pos_ref, f32[512,512]{1,0:T(8,128)} %get-tuple-element.40.refs_0_, f32[512,512]{1,0:T(8,128)} %copy-done.17), custom_call_target="tpu_custom_call" | custom-call | flops 1073741824 | bytes 4194304 | tf_op jit(solution)/shard_map/pallas_call | solution.py:95
  182.3 3.9 %all-to-all-start.3 = ((f32[8,2,64,512]{3,2,1,0:T(8,128)}), f32[8,2,64,512]{3,2,1,0:T(8,128)S(1)}, u32[]{:S(2)}, u32[]{:S(2)}) async-start(f32[8,2,64,512]{3,2,1,0:T(8,128)} %bitcast.58), calls=%async_computation.3 | async-start | bytes 4194304 | tf_op jit(solution)/shard_map/all_to_all | solution.py:241
  186.2 11.4 %shard_map.41 = (f32[512,256]{1,0:T(8,128)}, f32[512,256]{1,0:T(8,128)}) custom-call(s32[8,16]{1,0:T(8,128)} %convert_reduce_fusion.present_ref, s32[1,4096]{1,0:T(1,128)} %fusion.14.pos_ref, f32[512,4096]{1,0:T(8,128)} %counts_ref.9), custom_call_target="tpu_custom_call" | custom-call | flops 2147483648 | bytes 9437184 | tf_op jit(solution)/shard_map/pallas_call | solution.py:64
  199.6 1.1 reduce-window.26
  201.0 11.1 %collective-permute-done.refs_1_ = f32[512,256]{1,0:T(8,128)S(1)} collective-permute-done((f32[512,256]{1,0:T(8,128)}, f32[512,256]{1,0:T(8,128)S(1)}, u32[]{:S(2)}, u32[]{:S(2)}) %collective-permute-start) | collective-permute-done | bytes 524320 | tf_op jit(solution)/shard_map/ppermute | solution.py:238
  212.1 0.8 copy-done.19
  212.9 2.9 shard_map.42
  215.9 3.8 %all-to-all-start.2 = ((f32[8,2,64,256]{3,2,1,0:T(8,128)}), f32[8,2,64,256]{3,2,1,0:T(8,128)S(1)}, u32[]{:S(2)}, u32[]{:S(2)}) async-start(f32[8,2,64,256]{3,2,1,0:T(8,128)} %bitcast.61), calls=%async_computation.2 | async-start | bytes 2097152 | tf_op jit(solution)/shard_map/all_to_all | solution.py:241
  219.7 1.1 reduce-window.24
  222.7 3.1 shard_map.55
  225.8 2.6 collective-permute-start.9
  228.4 3.1 shard_map.54
  231.9 3.2 shard_map.53
  235.1 2.6 collective-permute-start.7
  237.7 2.6 shard_map.51
  240.6 1.0 copy-done.3
  241.6 2.6 shard_map.52
  244.1 2.6 collective-permute-start.6
  246.8 76.5 %all_to_all.31 = f32[16,1,2048]{2,1,0:T(1,128)S(1)} all-to-all(f32[16,1,2048]{2,1,0:T(1,128)S(1)} %broadcast_in_dim.23), channel_id=1, replica_groups=mesh['blk'=16,'col'=2] {'blk'}, dimensions={0} | all-to-all | bytes 262144 | tf_op jit(solution)/shard_map/all_to_all | solution.py:249
  325.2 4.2 %shard_map.56 = (f32[256,2048]{1,0:T(8,128)}, f32[256,128]{1,0:T(8,128)}, f32[256,128]{1,0:T(8,128)}) custom-call(f32[1,2048]{1,0:T(1,128)} %bitcast.63, f32[256,256]{1,0:T(8,128)} %get-tuple-element.56.refs_0_, f32[256,512]{1,0:T(8,128)} %get-tuple-element.58.refs_1_, f32[256,512]{1,0:T(8,128)} %get-tuple-element.60.refs_2_, ...), custom_call_target="tpu_custom_call" | custom-call | flops 9175040 | bytes 5505024 | tf_op jit(solution)/shard_map/pallas_call | solution.py:154
  330.1 1.9 shard_map.57
  332.9 3.1 collective-permute-done.10
  (85 shorter events, 12.1 us)
Async XLA Ops:
  3.7 12.9 %copy-start.9 = (s32[8192,1]{0,1:T(1,128)S(1)}, s32[8192,1]{0,1:T(1,128)}, u32[]{:S(2)}) copy-start(s32[8192,1]{0,1:T(1,128)} %param.3) | copy-start | bytes 98308
  15.0 14.5 %collective-permute-start.4 = (f32[512,256]{1,0:T(8,128)}, f32[512,256]{1,0:T(8,128)S(1)}, u32[]{:S(2)}, u32[]{:S(2)}) collective-permute-start(f32[512,256]{1,0:T(8,128)} %get-tuple-element.50), channel_id=1, source_target_pairs={{0,1},{1,0},{2,3},{3,2},{4,5},{5,4},{6,7},{7,6},{8,9},{9,8},{10,11... | collective-permute-start | bytes 1572872 | tf_op jit(solution)/shard_map/ppermute | solution.py:238
  29.6 0.8 copy-start.18
  33.3 49.2 %all-to-all-start.1 = ((f32[8,2,64,256]{3,2,1,0:T(8,128)}), f32[8,2,64,256]{3,2,1,0:T(8,128)S(1)}, u32[]{:S(2)}, u32[]{:S(2)}) async-start(f32[8,2,64,256]{3,2,1,0:T(8,128)} %bitcast.62), calls=%async_computation.1 | async-start | bytes 2097152 | tf_op jit(solution)/shard_map/all_to_all | solution.py:241
  52.0 25.7 %collective-permute-start.3 = (f32[512,512]{1,0:T(8,128)}, f32[512,512]{1,0:T(8,128)S(1)}, u32[]{:S(2)}, u32[]{:S(2)}) collective-permute-start(f32[512,512]{1,0:T(8,128)} %get-tuple-element.47), channel_id=1, source_target_pairs={{0,1},{1,0},{2,3},{3,2},{4,5},{5,4},{6,7},{7,6},{8,9},{9,8},{10,11... | collective-permute-start | bytes 3145736 | tf_op jit(solution)/shard_map/ppermute | solution.py:238
  77.7 1.0 copy-start.15
  82.5 1.0 copy-start.2
  83.5 48.1 %all-to-all-start.5 = ((f32[8,2,64,512]{3,2,1,0:T(8,128)}), f32[8,2,64,512]{3,2,1,0:T(8,128)S(1)}, u32[]{:S(2)}, u32[]{:S(2)}) async-start(f32[8,2,64,512]{3,2,1,0:T(8,128)} %bitcast.59), calls=%async_computation.5 | async-start | bytes 4194304 | tf_op jit(solution)/shard_map/all_to_all | solution.py:241
  100.4 26.2 %collective-permute-start.2 = (f32[512,512]{1,0:T(8,128)}, f32[512,512]{1,0:T(8,128)S(1)}, u32[]{:S(2)}, u32[]{:S(2)}) collective-permute-start(f32[512,512]{1,0:T(8,128)} %get-tuple-element.44), channel_id=1, source_target_pairs={{0,1},{1,0},{2,3},{3,2},{4,5},{5,4},{6,7},{7,6},{8,9},{9,8},{10,11... | collective-permute-start | bytes 3145736 | tf_op jit(solution)/shard_map/ppermute | solution.py:238
  126.7 1.0 copy-start.16
  131.6 1.3 copy-start
  132.9 49.4 %all-to-all-start.4 = ((f32[8,2,64,512]{3,2,1,0:T(8,128)}), f32[8,2,64,512]{3,2,1,0:T(8,128)}, u32[]{:S(2)}, u32[]{:S(2)}) async-start(f32[8,2,64,512]{3,2,1,0:T(8,128)} %bitcast.60), calls=%async_computation.4 | async-start | bytes 4194304 | tf_op jit(solution)/shard_map/all_to_all | solution.py:241
  150.3 27.1 %collective-permute-start.1 = (f32[512,512]{1,0:T(8,128)}, f32[512,512]{1,0:T(8,128)S(1)}, u32[]{:S(2)}, u32[]{:S(2)}) collective-permute-start(f32[512,512]{1,0:T(8,128)} %get-tuple-element.41), channel_id=1, source_target_pairs={{0,1},{1,0},{2,3},{3,2},{4,5},{5,4},{6,7},{7,6},{8,9},{9,8},{10,11... | collective-permute-start | bytes 3145736 | tf_op jit(solution)/shard_map/ppermute | solution.py:238
  177.4 1.1 copy-start.17
  182.3 33.5 %all-to-all-start.3 = ((f32[8,2,64,512]{3,2,1,0:T(8,128)}), f32[8,2,64,512]{3,2,1,0:T(8,128)S(1)}, u32[]{:S(2)}, u32[]{:S(2)}) async-start(f32[8,2,64,512]{3,2,1,0:T(8,128)} %bitcast.58), calls=%async_computation.3 | async-start | bytes 4194304 | tf_op jit(solution)/shard_map/all_to_all | solution.py:241
  197.6 14.5 %collective-permute-start = (f32[512,256]{1,0:T(8,128)}, f32[512,256]{1,0:T(8,128)S(1)}, u32[]{:S(2)}, u32[]{:S(2)}) collective-permute-start(f32[512,256]{1,0:T(8,128)} %get-tuple-element.38), channel_id=1, source_target_pairs={{0,1},{1,0},{2,3},{3,2},{4,5},{5,4},{6,7},{7,6},{8,9},{9,8},{10,11... | collective-permute-start | bytes 1572872 | tf_op jit(solution)/shard_map/ppermute | solution.py:238
  212.1 0.8 copy-start.19
  212.9 9.7 %copy-start.12 = (f32[1,512]{1,0:T(1,128)S(1)}, f32[1,512]{1,0:T(1,128)}, u32[]{:S(2)}) copy-start(f32[1,512]{1,0:T(1,128)} %get-tuple-element.42) | copy-start | bytes 6148
  215.8 6.8 %copy-start.14 = (f32[1,256]{1,0:T(1,128)S(1)}, f32[1,256]{1,0:T(1,128)}, u32[]{:S(2)}) copy-start(f32[1,256]{1,0:T(1,128)} %get-tuple-element.39) | copy-start | bytes 3076
  215.8 10.0 %copy-start.1 = (f32[8,2,64,512]{3,2,1,0:T(8,128)}, f32[8,2,64,512]{3,2,1,0:T(8,128)S(1)}, u32[]{:S(2)}) copy-start(f32[8,2,64,512]{3,2,1,0:T(8,128)S(1)} %all-to-all-done.3.got_ref) | copy-start | bytes 6291460
  215.9 24.7 %all-to-all-start.2 = ((f32[8,2,64,256]{3,2,1,0:T(8,128)}), f32[8,2,64,256]{3,2,1,0:T(8,128)S(1)}, u32[]{:S(2)}, u32[]{:S(2)}) async-start(f32[8,2,64,256]{3,2,1,0:T(8,128)} %bitcast.61), calls=%async_computation.2 | async-start | bytes 2097152 | tf_op jit(solution)/shard_map/all_to_all | solution.py:241
  225.8 11.9 %copy-start.11 = (f32[1,512]{1,0:T(1,128)S(1)}, f32[1,512]{1,0:T(1,128)}, u32[]{:S(2)}) copy-start(f32[1,512]{1,0:T(1,128)} %get-tuple-element.45) | copy-start | bytes 6148
  225.8 11.9 %copy-start.10 = (f32[1,512]{1,0:T(1,128)S(1)}, f32[1,512]{1,0:T(1,128)}, u32[]{:S(2)}) copy-start(f32[1,512]{1,0:T(1,128)} %get-tuple-element.48) | copy-start | bytes 6148
  225.8 98.2 %collective-permute-start.9 = (f32[256,512]{1,0:T(8,128)}, f32[256,512]{1,0:T(8,128)S(1)}, u32[]{:S(2)}, u32[]{:S(2)}) collective-permute-start(f32[256,512]{1,0:T(8,128)} %get-tuple-element.66), channel_id=1, source_target_pairs={{0,16},{2,18},{4,20},{6,22},{8,24},{10,26},{12,28},{14,30},{16,0},... | collective-permute-start | bytes 1572872 | tf_op jit(solution)/shard_map/ppermute | solution.py:246
  231.6 15.1 %copy-start.13 = (f32[1,256]{1,0:T(1,128)S(1)}, f32[1,256]{1,0:T(1,128)}, u32[]{:S(2)}) copy-start(f32[1,256]{1,0:T(1,128)} %get-tuple-element.51) | copy-start | bytes 3076
  231.6 92.4 %collective-permute-start.8 = (f32[256,512]{1,0:T(8,128)}, f32[256,512]{1,0:T(8,128)S(1)}, u32[]{:S(2)}, u32[]{:S(2)}) collective-permute-start(f32[256,512]{1,0:T(8,128)} %get-tuple-element.65), channel_id=1, source_target_pairs={{0,16},{2,18},{4,20},{6,22},{8,24},{10,26},{12,28},{14,30},{16,0},... | collective-permute-start | bytes 1572872 | tf_op jit(solution)/shard_map/ppermute | solution.py:246
  235.1 88.9 %collective-permute-start.7 = (f32[256,512]{1,0:T(8,128)}, f32[256,512]{1,0:T(8,128)S(1)}, u32[]{:S(2)}, u32[]{:S(2)}) collective-permute-start(f32[256,512]{1,0:T(8,128)} %get-tuple-element.64), channel_id=1, source_target_pairs={{0,16},{2,18},{4,20},{6,22},{8,24},{10,26},{12,28},{14,30},{16,0},... | collective-permute-start | bytes 1572872 | tf_op jit(solution)/shard_map/ppermute | solution.py:246
  240.2 89.2 %collective-permute-start.5 = (f32[256,256]{1,0:T(8,128)}, f32[256,256]{1,0:T(8,128)S(1)}, u32[]{:S(2)}, u32[]{:S(2)}) collective-permute-start(f32[256,256]{1,0:T(8,128)} %get-tuple-element.54), channel_id=1, source_target_pairs={{0,16},{2,18},{4,20},{6,22},{8,24},{10,26},{12,28},{14,30},{16,0},... | collective-permute-start | bytes 786440 | tf_op jit(solution)/shard_map/ppermute | solution.py:246
  240.6 1.0 copy-start.3
  244.1 79.8 %collective-permute-start.6 = (f32[256,256]{1,0:T(8,128)}, f32[256,256]{1,0:T(8,128)S(1)}, u32[]{:S(2)}, u32[]{:S(2)}) collective-permute-start(f32[256,256]{1,0:T(8,128)} %get-tuple-element.63), channel_id=1, source_target_pairs={{0,16},{2,18},{4,20},{6,22},{8,24},{10,26},{12,28},{14,30},{16,0},... | collective-permute-start | bytes 786440 | tf_op jit(solution)/shard_map/ppermute | solution.py:246
  324.0 0.7 copy-start.7
  324.0 0.9 copy-start.4
  324.0 1.1 copy-start.5
  324.0 1.2 copy-start.6
  329.4 0.7 copy-start.8
  332.1 3.9 %collective-permute-start.10 = (f32[8,256]{1,0:T(8,128)}, f32[8,256]{1,0:T(8,128)S(1)}, u32[]{:S(2)}, u32[]{:S(2)}) collective-permute-start(f32[8,256]{1,0:T(8,128)} %get-tuple-element.71), channel_id=1, source_target_pairs={{0,1},{1,0},{2,3},{3,2},{4,5},{5,4},{6,7},{7,6},{8,9},{9,8},{10,11... | collective-permute-start | bytes 24584 | tf_op jit(solution)/shard_map/ppermute | solution.py:256

commit v2 on v1

v2 whole, which is shorter than its diff:
```python
import functools

import jax
import jax.numpy as jnp
from jax import lax
from jax.experimental import pallas as pl
from jax.experimental.pallas import tpu as pltpu
from jax.sharding import PartitionSpec as P

PARTS = (2, 4, 4, 4, 2)
VMEM = 24 * 2**20
F32, BF16, I32 = jnp.float32, jnp.bfloat16, jnp.int32


def widths(owned_cols):
    unit = owned_cols // sum(PARTS)
    return [p * unit for p in PARTS] if unit % 128 == 0 else [owned_cols]


def split(x):
    hi = x.astype(BF16)
    return hi, (x - hi.astype(F32)).astype(BF16)


def hot(labels, count, base=0):
    index = lax.broadcasted_iota(I32, (count, labels.shape[1]), 0) + base
    return jnp.where(index == labels, 1.0, 0.0).astype(BF16)


def mxu(a, b, dims):
    return lax.dot_general(a, b, (dims, ((), ())), preferred_element_type=F32)


def call(kernel, flops, nbytes, **kw):
    return pl.pallas_call(
        kernel,
        cost_estimate=pl.CostEstimate(flops=flops, bytes_accessed=nbytes, transcendentals=0),
        compiler_params=pltpu.CompilerParams(vmem_limit_bytes=VMEM),
        **kw,
    )


def columns_kernel(start, owned, first, present_ref, pos_ref, x_ref, *refs):
    sources = present_ref.shape[0]
    tile = x_ref.shape[1] // sources
    halves_ref, out_refs = (refs[0], refs[1:]) if first else (x_ref, refs)
    rows, width = out_refs[0].shape
    per_column = present_ref.shape[1] // len(out_refs)
    for out_ref in out_refs:
        out_ref[...] = jnp.zeros_like(out_ref)

    def step(k, carry):
        at = pl.ds(pl.multiple_of(k * tile, tile), tile)
        if first:
            halves_ref[:rows, at], halves_ref[rows:, at] = split(x_ref[:, at])
        for c, out_ref in enumerate(out_refs):
            for b in range(width // owned):
                block = c * per_column + start // owned + b

                @pl.when(present_ref[k, block] > 0)
                def _():
                    part = mxu(halves_ref[:, at], hot(pos_ref[:, at], owned, block * owned), ((1,), (1,)))
                    out_ref[:, b * owned : (b + 1) * owned] += part[:rows] + part[rows:]

        return carry

    lax.fori_loop(0, sources, step, 0)


def merge_columns(x, pos, present, owned, columns, start, width, first):
    rows, cols = x.shape if first else (x.shape[0] // 2, x.shape[1])
    vmem = pl.BlockSpec(memory_space=pltpu.VMEM)
    halves = [jax.ShapeDtypeStruct((2 * rows, cols), BF16)] if first else []
    return call(
        functools.partial(columns_kernel, start, owned, first),
        2 * rows * cols * columns * width, 4 * rows * (cols + columns * width),
        in_specs=[pl.BlockSpec(memory_space=pltpu.SMEM), vmem, vmem],
        out_specs=[vmem] * (len(halves) + columns),
        out_shape=halves + [jax.ShapeDtypeStruct((rows, width), F32)] * columns,
    )(present, pos, x)


def slots_kernel(carrier, pos_ref, *refs):
    ins, out_ref, sum_ref, table = refs[:-3], refs[-3], refs[-2], refs[-1]
    known_ref, ins = (ins[0], ins[1:]) if carrier is not None else (None, ins)
    peers, depth, tile = out_ref.shape
    used = table.shape[0] // peers

    @pl.when(pl.program_id(0) == 0)
    def _():
        table[...] = hot(pos_ref[...], table.shape[0])

    total = ins[0][...]
    for ref in ins[1:]:
        total += ref[...]
    column_sum = jnp.sum(total, axis=0, keepdims=True)
    sum_ref[...] = column_sum
    hi, lo = split(total)
    filled = mxu(table[...], hi, ((1,), (0,))) + mxu(table[...], lo, ((1,), (0,)))
    out_ref[:, :used] = filled.reshape(peers, used, tile)
    if carrier is not None:
        row = lax.broadcasted_iota(I32, known_ref.shape, 0)
        sums = jnp.where(row == carrier, column_sum, known_ref[...])
        out_ref[:, used:] = jnp.broadcast_to(sums[None], (peers, depth - used, tile))


def fill_slots(pos, ins, peers, slots, carrier=None, known=None):
    rows, width = ins[0].shape
    tile = min(width, 256)
    depth = slots // peers + (0 if carrier is None else 8)
    extra = [] if carrier is None else [known]
    return call(
        functools.partial(slots_kernel, carrier),
        4 * slots * rows * width, 4 * width * (rows * len(ins) + slots),
        grid=(width // tile,),
        in_specs=[pl.BlockSpec((1, rows), lambda k: (0, 0))]
        + [pl.BlockSpec((8, tile), lambda k: (0, k))] * len(extra)
        + [pl.BlockSpec((rows, tile), lambda k: (0, k))] * len(ins),
        out_specs=[pl.BlockSpec((peers, depth, tile), lambda k: (0, 0, k)), pl.BlockSpec((1, tile), lambda k: (0, k))],
        out_shape=[jax.ShapeDtypeStruct((peers, depth, width), F32), jax.ShapeDtypeStruct((1, width), F32)],
        scratch_shapes=[pltpu.VMEM((slots, rows), BF16)],
    )(pos, *extra, *ins)


def rows_kernel(pos_ref, got_ref, keep_ref, send_ref, *sum_refs):
    peers, _, tile = got_ref.shape
    owned, cap = keep_ref.shape[0], pos_ref.shape[1] // peers
    for side, ref in enumerate((keep_ref, send_ref)):
        hi, lo = split(got_ref[:, side * cap : (side + 1) * cap].reshape(peers * cap, tile))
        table = hot(pos_ref[side : side + 1, :], owned)
        ref[:owned] = mxu(table, hi, ((1,), (0,))) + mxu(table, lo, ((1,), (0,)))
    for ref in sum_refs:
        ref[...] = jnp.sum(got_ref[:, 2 * cap :], axis=0)
        send_ref[owned:] = ref[...]


def merge_rows(pos, got, owned, carrier):
    peers, depth, width = got.shape
    slots = pos.shape[1]
    tile = min(width, 256)
    heights = [owned, owned + 8, 8] if carrier else [owned, owned]
    return call(
        rows_kernel, 8 * owned * slots * width, 4 * width * (2 * owned + 2 * slots),
        grid=(width // tile,),
        in_specs=[pl.BlockSpec((2, slots), lambda k: (0, 0)), pl.BlockSpec((peers, depth, tile), lambda k: (0, 0, k))],
        out_specs=[pl.BlockSpec((h, tile), lambda k: (0, k)) for h in heights],
        out_shape=[jax.ShapeDtypeStruct((h, width), F32) for h in heights],
    )(pos, got)


def fold(x):
    return sum(x[:, j : j + 128] for j in range(0, x.shape[1], 128))


def terms(block, in_total, new):
    return fold(block * jnp.log(block * (new / in_total))), fold(block)


def early_kernel(plan, new, in_total_ref, *refs):
    ins, (merged_ref, logs_ref, out_ref) = list(refs[:-3]), refs[-3:]
    start, logs, out = 0, 0.0, 0.0
    for q, (width, parts) in enumerate(plan):
        block = sum(ins.pop(0)[...] for _ in range(parts))
        merged_ref[:, start : start + width] = block
        more = terms(block, in_total_ref[q : q + 1, :width], new)
        logs, out, start = logs + more[0], out + more[1], start + width
    logs_ref[...], out_ref[...] = logs, out


def finish_early(plan, new, in_total, chunks):
    owned, total, done = chunks[0][0].shape[0], sum(plan), sum(plan[:-1])
    tile = min(owned, 64)
    lanes = pl.BlockSpec((tile, 128), lambda k: (k, 0))
    return call(
        functools.partial(early_kernel, [(w, len(c)) for w, c in zip(plan, chunks)], new),
        20 * owned * done, 12 * owned * done,
        grid=(owned // tile,),
        in_specs=[pl.BlockSpec(in_total.shape, lambda k: (0, 0))]
        + [pl.BlockSpec((tile, w), lambda k: (k, 0)) for w, c in zip(plan, chunks) for _ in c],
        out_specs=[pl.BlockSpec((tile, done), lambda k: (k, 0)), lanes, lanes],
        out_shape=[jax.ShapeDtypeStruct((owned, total), F32)] + [jax.ShapeDtypeStruct((owned, 128), F32)] * 2,
    )(in_total, *(x for c in chunks for x in c))


def last_kernel(chunk, new, in_total_ref, keep_ref, other_ref, *refs):
    merged_ref, part_ref = refs[-2:]
    block = keep_ref[...] + other_ref[...]
    merged_ref[...] = block
    logs, out = terms(block, in_total_ref[chunk : chunk + 1, : block.shape[1]], new)
    if len(refs) > 2:
        logs, out = logs + refs[1][...], out + refs[2][...]
    row = lax.broadcasted_iota(I32, part_ref.shape, 0)
    logs = jnp.sum(logs.T, axis=0, keepdims=True)
    out = jnp.sum(out.T, axis=0, keepdims=True)
    total = jnp.sum(jnp.sum(in_total_ref[...], axis=0, keepdims=True), axis=1, keepdims=True)
    part_ref[...] = jnp.where(row == 0, logs, jnp.where(row == 1, out, total))


def finish_last(plan, new, in_total, keep, other, early):
    owned, width, total = keep.shape[0], plan[-1], sum(plan)
    at = (total - width) // width
    whole = pl.BlockSpec((owned, width), lambda k: (0, 0))
    lanes = [pl.BlockSpec((owned, 128), lambda k: (0, 0))] * 2
    return call(
        functools.partial(last_kernel, len(plan) - 1, new), 20 * owned * width, 12 * owned * width,
        grid=(1,),
        in_specs=[pl.BlockSpec(in_total.shape, lambda k: (0, 0)), whole, whole]
        + ([pl.BlockSpec(memory_space=pl.ANY)] + lanes if early else []),
        out_specs=[pl.BlockSpec((owned, width), lambda k: (0, at)), pl.BlockSpec((8, owned), lambda k: (0, 0))],
        out_shape=[jax.ShapeDtypeStruct((owned, total), F32), jax.ShapeDtypeStruct((8, owned), F32)],
        input_output_aliases={3: 0} if early else {},
    )(in_total, keep, other, *early)


def tags_of(ids, mine, capacity):
    rank = jnp.cumsum(mine.astype(I32), axis=1) - 1
    hit = mine[:, None, :] & (rank[:, None, :] == jnp.arange(capacity, dtype=I32)[None, :, None])
    return jnp.max(jnp.where(hit, ids[:, None, :], -1), axis=2)


def body(counts, merge_map):
    rows, cols = counts.shape
    groups, columns = lax.axis_size("blk"), lax.axis_size("col")
    blk, col = lax.axis_index("blk"), lax.axis_index("col")
    ids = merge_map[:, 0]
    new = ids.shape[0] // 2
    owned, owned_cols = new // groups, new // columns
    fanout = min(groups // 2, rows // 2)
    cap = rows // fanout
    half = groups // 2
    plan = widths(owned_cols)
    starts = [sum(plan[:q]) for q in range(len(plan))]
    row_labels = lax.dynamic_slice_in_dim(ids, blk * rows, rows, 0)
    col_labels = lax.dynamic_slice_in_dim(ids, col * cols, cols, 0)

    step_of = lax.rem(col_labels // owned_cols - col + columns, columns)
    col_pos = step_of * owned_cols + lax.rem(col_labels, owned_cols)
    mapped = (col_pos // owned).reshape(cols // rows, rows, 1) == jnp.arange(groups, dtype=I32)
    present = jnp.max(mapped.astype(I32), axis=1)

    owner = row_labels // owned
    table = (owner[:, None] == jnp.arange(groups, dtype=I32)[None, :]).astype(I32)
    rank = jnp.sum(jnp.cumsum(table, axis=0) * table, axis=1) - 1
    place = lax.rem(owner, half) * 2 + (owner // half != blk // half).astype(I32)
    row_pos = (place * cap + rank)[None, :]

    base = (blk // half) * half
    peers = lax.dynamic_slice_in_dim(ids.reshape(groups, rows), base, half, 0)
    take_pos = []
    for agg in (blk, lax.rem(blk + half, groups)):
        tags = tags_of(peers, peers // owned == agg, cap).reshape(-1)
        take_pos.append(jnp.where(tags < 0, -1, tags - agg * owned))
    take_pos = jnp.stack(take_pos)

    n = len(plan)
    carrier = max(n - 2, 0)
    keeps, others, halves, arrived = [], [], counts, []
    for q, width in enumerate(plan):
        parts = list(merge_columns(halves, col_pos[None, :], present, owned, columns, starts[q], width, q == 0))
        if q == 0:
            halves = parts.pop(0)
        for step in range(1, columns):
            parts[step] = lax.ppermute(parts[step], "col", [(i, (i + step) % columns) for i in range(columns)])
        arrived.append(parts)
    slotted, sums = [None] * n, [jnp.zeros((1, plan[carrier]), F32)] * 8
    for q in [i for i in range(n) if i != carrier]:
        slotted[q], column_sum = fill_slots(row_pos, arrived[q], half, groups * cap)
        sums[q] = jnp.pad(column_sum, ((0, 0), (0, plan[carrier] - plan[q])))
    known = jnp.concatenate(sums, axis=0)
    slotted[carrier], _ = fill_slots(row_pos, arrived[carrier], half, groups * cap, carrier, known)
    for q in range(n):
        got = lax.all_to_all(
            slotted[q], "blk", split_axis=0, concat_axis=0, tiled=True,
            axis_index_groups=[list(range(half)), list(range(half, groups))],
        )
        keep, send, *half_sums = merge_rows(take_pos, got, owned, q == carrier)
        others.append(lax.ppermute(send, "blk", [(i, (i + half) % groups) for i in range(groups)]))
        keeps.append(keep)
        if half_sums:
            in_total = half_sums[0] + others[q][owned:]
    chunks = list(zip(keeps, others))
    for q in range(max(min(2, n - 3), 0)):
        chunks[q] = (keeps[q] + others[q],)
    early = ()
    if n > 1:
        early = finish_early(plan, new, in_total, chunks[:-1])
    merged, part = finish_last(plan, new, in_total, keeps[-1], others[-1], early)
    if columns == 2:
        part += lax.ppermute(part, "col", [(0, 1), (1, 0)])
    else:
        part = lax.psum(part, "col")
    block_terms = part[0] / part[1] + jnp.log(part[2] / (part[1] * new))
    return (merged, block_terms)


def solution(mesh):
    placed = (P("blk", "col"), P())
    return jax.shard_map(body, mesh=mesh, in_specs=placed, out_specs=(P("blk", "col"), P("blk")), check_vma=False)
```

time: 339 us -> 328 us (0.968)
  waiting for transfers between devices: 98 us -> 190 us
  blocking collectives: 76.5 us -> 0 us
  Pallas kernels: 101 us -> 60.2 us
  local copies, waits for them, and re-layouts: 12.1 us -> 28.2 us
    all_to_all x1 -> x0, blocking collectives: 76.5 us -> none  [body(): sums = lax.all_to_all(sums, 'blk', split_axis=0, concat_axis=0, tiled=True)]
    ppermute x5, waiting for transfers between devices: 0.01 us -> 71.6 us  [body(): lax.ppermute(send, 'blk', [(i, (i + half) % groups) for i in range(groups)])]
    pallas_call x17, Pallas kernels: 101 us -> 60.2 us  [the longest x5 37 us: merge_columns(): call(functools.partial(columns_kernel, start, owned, first), 2 * rows * c...]
    all_to_all x5, waiting for transfers between devices: 0.01 us -> 28.7 us  [body(): lax.all_to_all(slotted[q], 'blk', split_axis=0, concat_axis=0, tiled=True...]
    unnamed x45 -> x33, local copies, waits for them, and re-layouts: 10.4 us -> 26.6 us
    ppermute x5, waiting for transfers between devices: 94.9 us -> 87.7 us  [body(): lax.ppermute(parts[step], 'col', [(i, (i + step) % columns) for i in rang...]
  transfers between devices with their start and end apart: 16 -> 16, of which waited for: 6 -> 8; matrix products, arithmetic and copies ran while one was open for 3% -> 3% of each run, Pallas kernels for 25% -> 16%
where the time goes in v2:
time: 328 us; the launch traced here: 327 us
  waiting for transfers between devices  190 us (58%)
  Pallas kernels  60.2 us (18%)
  starting transfers between devices  38.4 us (12%)
  local copies, waits for them, and re-layouts  28.2 us (9%)
  other arithmetic  9.09 us (3%)
    ppermute x5, waiting for transfers between devices, body(): lax.ppermute(parts[step], 'col', [(i, (i + step) % columns) for i in rang...  87.7 us
    ppermute x5, waiting for transfers between devices, body(): lax.ppermute(send, 'blk', [(i, (i + half) % groups) for i in range(groups)])  71.6 us
    pallas_call x5, Pallas kernels, merge_columns(): call(functools.partial(columns_kernel, start, owned, first), 2 * rows * c...  37 us
    all_to_all x5, waiting for transfers between devices, body(): lax.all_to_all(slotted[q], 'blk', split_axis=0, concat_axis=0, tiled=True...  28.7 us
    unnamed x33, local copies, waits for them, and re-layouts  26.6 us
    all_to_all x5, starting transfers between devices, body(): lax.all_to_all(slotted[q], 'blk', split_axis=0, concat_axis=0, tiled=True...  21.1 us
    pallas_call x5, Pallas kernels, merge_rows(): call(rows_kernel, 8 * owned * slots * width, 4 * width * (2 * owned + 2 *...  9.97 us
    ppermute x5, starting transfers between devices, body(): lax.ppermute(parts[step], 'col', [(i, (i + step) % columns) for i in rang...  9.72 us
  transfers between devices with their start and end apart: 16, of which 8 were waited for; matrix products, arithmetic and copies ran while one was open for 3% of the time, Pallas kernels for 16%

profile of v2, /device:TPU:0, one launch (start us, length us, event | category | flops | bytes accessed | tf_op | source)
XLA Modules:
  0.0 326.9 jit_solution(2928530668429922480)
XLA Ops:
  2.5 3.4 %copy-done = f32[512,4096]{1,0:T(8,128)S(1)} copy-done((f32[512,4096]{1,0:T(8,128)S(1)}, f32[512,4096]{1,0:T(8,128)}, u32[]{:S(2)}) %copy-start) | copy-done | bytes 8388632
  5.9 6.2 %shard_map.41 = (bf16[1024,4096]{1,0:T(8,128)(2,1)S(1)}, f32[512,256]{1,0:T(8,128)S(1)}, f32[512,256]{1,0:T(8,128)S(1)}) custom-call(s32[8,16]{1,0:T(8,128)S(1)} %convert_reduce_fusion.present_ref, s32[1,4096]{1,0:T(1,128)S(1)} %fusion.14.pos_ref, f32[512,4096]{1,0:T(8,128)S(1)} %copy-done), custom_call_target="tpu_custom_call" | custom-call | flops 2147483648 | bytes 9437184 | tf_op jit(solution)/shard_map/pallas_call | solution.py:74
  12.2 3.2 copy-done.1
  15.4 2.0 collective-permute-start
  17.4 1.2 reduce-window.26
  19.0 10.7 %collective-permute-done.refs_1_ = f32[512,256]{1,0:T(8,128)S(1)} collective-permute-done((f32[512,256]{1,0:T(8,128)S(1)}, f32[512,256]{1,0:T(8,128)S(1)}, u32[]{:S(2)}, u32[]{:S(2)}) %collective-permute-start) | collective-permute-done | bytes 524320 | tf_op jit(solution)/shard_map/ppermute | solution.py:263
  29.7 1.8 shard_map.42
  31.5 4.6 %all-to-all-start.2 = ((f32[8,128,256]{2,1,0:T(8,128)}), f32[8,128,256]{2,1,0:T(8,128)S(1)}, u32[]{:S(2)}, u32[]{:S(2)}) async-start(f32[8,128,256]{2,1,0:T(8,128)} %get-tuple-element.59), calls=%async_computation.2 | async-start | bytes 2097152 | tf_op jit(solution)/shard_map/all_to_all | solution.py:272
  36.1 3.4 %copy-done.2 = bf16[1024,4096]{1,0:T(8,128)(2,1)S(1)} copy-done((bf16[1024,4096]{1,0:T(8,128)(2,1)S(1)}, bf16[1024,4096]{1,0:T(8,128)(2,1)}, u32[]{:S(2)}) %copy-start.2) | copy-done | bytes 8388632
  39.5 8.1 %shard_map.43 = (f32[512,512]{1,0:T(8,128)S(1)}, f32[512,512]{1,0:T(8,128)S(1)}) custom-call(s32[8,16]{1,0:T(8,128)S(1)} %convert_reduce_fusion.present_ref, s32[1,4096]{1,0:T(1,128)S(1)} %fusion.14.pos_ref, bf16[1024,4096]{1,0:T(8,128)(2,1)S(1)} %copy-done.2), custom_call_target="tpu_custom_call" | custom-call | flops 4294967296 | bytes 10485760 | tf_op jit(solution)/shard_map/pallas_call | solution.py:74
  47.6 1.5 collective-permute-start.1
  49.1 24.1 %collective-permute-done.1.refs_1_ = f32[512,512]{1,0:T(8,128)S(1)} collective-permute-done((f32[512,512]{1,0:T(8,128)S(1)}, f32[512,512]{1,0:T(8,128)S(1)}, u32[]{:S(2)}, u32[]{:S(2)}) %collective-permute-start.1) | collective-permute-done | bytes 1048608 | tf_op jit(solution)/shard_map/ppermute | solution.py:263
  73.2 2.0 shard_map.44
  75.2 1.3 copy-done.9
  76.5 3.8 %all-to-all-start.3 = ((f32[8,128,512]{2,1,0:T(8,128)}), f32[8,128,512]{2,1,0:T(8,128)S(1)}, u32[]{:S(2)}, u32[]{:S(2)}) async-start(f32[8,128,512]{2,1,0:T(8,128)} %copy-done.9), calls=%async_computation.3 | async-start | bytes 4194304 | tf_op jit(solution)/shard_map/all_to_all | solution.py:272
  80.3 3.4 %copy-done.3 = bf16[1024,4096]{1,0:T(8,128)(2,1)S(1)} copy-done((bf16[1024,4096]{1,0:T(8,128)(2,1)S(1)}, bf16[1024,4096]{1,0:T(8,128)(2,1)}, u32[]{:S(2)}) %copy-start.3) | copy-done | bytes 8388632
  83.7 7.6 %shard_map.45 = (f32[512,512]{1,0:T(8,128)S(1)}, f32[512,512]{1,0:T(8,128)S(1)}) custom-call(s32[8,16]{1,0:T(8,128)S(1)} %convert_reduce_fusion.present_ref, s32[1,4096]{1,0:T(1,128)S(1)} %fusion.14.pos_ref, bf16[1024,4096]{1,0:T(8,128)(2,1)S(1)} %copy-done.3), custom_call_target="tpu_custom_call" | custom-call | flops 4294967296 | bytes 10485760 | tf_op jit(solution)/shard_map/pallas_call | solution.py:74
  91.3 3.4 %collective-permute-start.2 = (f32[512,512]{1,0:T(8,128)S(1)}, f32[512,512]{1,0:T(8,128)S(1)}, u32[]{:S(2)}, u32[]{:S(2)}) collective-permute-start(f32[512,512]{1,0:T(8,128)S(1)} %get-tuple-element.46), channel_id=1, source_target_pairs={{0,1},{1,0},{2,3},{3,2},{4,5},{5,4},{6,7},{7,6},{8,9},{9,8},{10,11... | collective-permute-start | bytes 3145736 | tf_op jit(solution)/shard_map/ppermute | solution.py:263
  94.7 23.8 %collective-permute-done.2.refs_1_ = f32[512,512]{1,0:T(8,128)S(1)} collective-permute-done((f32[512,512]{1,0:T(8,128)S(1)}, f32[512,512]{1,0:T(8,128)S(1)}, u32[]{:S(2)}, u32[]{:S(2)}) %collective-permute-start.2) | collective-permute-done | bytes 1048608 | tf_op jit(solution)/shard_map/ppermute | solution.py:263
  118.6 2.0 shard_map.46
  120.5 1.3 copy-done.8
  121.9 1.3 copy-done.5
  123.2 4.4 %all-to-all-start.4 = ((f32[8,128,512]{2,1,0:T(8,128)}), f32[8,128,512]{2,1,0:T(8,128)}, u32[]{:S(2)}, u32[]{:S(2)}) async-start(f32[8,128,512]{2,1,0:T(8,128)} %copy-done.8), calls=%async_computation.4 | async-start | bytes 4194304 | tf_op jit(solution)/shard_map/all_to_all | solution.py:272
  127.6 3.4 %copy-done.4 = bf16[1024,4096]{1,0:T(8,128)(2,1)S(1)} copy-done((bf16[1024,4096]{1,0:T(8,128)(2,1)S(1)}, bf16[1024,4096]{1,0:T(8,128)(2,1)}, u32[]{:S(2)}) %copy-start.4) | copy-done | bytes 8388632
  130.9 9.0 %shard_map.49 = (f32[512,512]{1,0:T(8,128)S(1)}, f32[512,512]{1,0:T(8,128)}) custom-call(s32[8,16]{1,0:T(8,128)S(1)} %convert_reduce_fusion.present_ref, s32[1,4096]{1,0:T(1,128)S(1)} %fusion.14.pos_ref, bf16[1024,4096]{1,0:T(8,128)(2,1)S(1)} %copy-done.4), custom_call_target="tpu_custom_call" | custom-call | flops 4294967296 | bytes 10485760 | tf_op jit(solution)/shard_map/pallas_call | solution.py:74
  141.0 2.7 collective-permute-start.4
  143.7 6.0 %shard_map.47 = (f32[512,256]{1,0:T(8,128)S(1)}, f32[512,256]{1,0:T(8,128)S(1)}) custom-call(s32[8,16]{1,0:T(8,128)S(1)} %convert_reduce_fusion.present_ref, s32[1,4096]{1,0:T(1,128)S(1)} %fusion.14.pos_ref, bf16[1024,4096]{1,0:T(8,128)(2,1)S(1)} %copy-done.4), custom_call_target="tpu_custom_call" | custom-call | flops 2147483648 | bytes 9437184 | tf_op jit(solution)/shard_map/pallas_call | solution.py:74
  149.8 29.1 %collective-permute-done.3.refs_1_ = f32[512,256]{1,0:T(8,128)S(1)} collective-permute-done((f32[512,256]{1,0:T(8,128)S(1)}, f32[512,256]{1,0:T(8,128)S(1)}, u32[]{:S(2)}, u32[]{:S(2)}) %collective-permute-start.3) | collective-permute-done | bytes 524320 | tf_op jit(solution)/shard_map/ppermute | solution.py:263
  180.6 1.2 copy-done.14
  181.8 2.5 shard_map.50
  184.4 1.4 copy-done.7
  185.7 3.8 %all-to-all-start = ((f32[8,136,512]{2,1,0:T(8,128)}), f32[8,136,512]{2,1,0:T(8,128)S(1)}, u32[]{:S(2)}, u32[]{:S(2)}) async-start(f32[8,136,512]{2,1,0:T(8,128)} %copy-done.7), calls=%async_computation | async-start | bytes 4456448 | tf_op jit(solution)/shard_map/all_to_all | solution.py:272
  190.8 1.1 reduce-window.24
  192.2 24.4 %all-to-all-done.got_ref = f32[8,136,512]{2,1,0:T(8,128)S(1)} async-done(((f32[8,136,512]{2,1,0:T(8,128)}), f32[8,136,512]{2,1,0:T(8,128)S(1)}, u32[]{:S(2)}, u32[]{:S(2)}) %all-to-all-start) | async-done | bytes 2228256 | tf_op jit(solution)/shard_map/all_to_all | solution.py:272
  216.7 4.4 %all-to-all-start.1 = ((f32[8,128,256]{2,1,0:T(8,128)}), f32[8,128,256]{2,1,0:T(8,128)}, u32[]{:S(2)}, u32[]{:S(2)}) async-start(f32[8,128,256]{2,1,0:T(8,128)} %copy-done.10), calls=%async_computation.1 | async-start | bytes 2097152 | tf_op jit(solution)/shard_map/all_to_all | solution.py:272
  221.1 1.1 reduce-window.20
  223.5 2.0 shard_map.51
  226.3 2.6 collective-permute-start.5
  228.9 1.9 shard_map.54
  231.2 3.0 shard_map.55
  234.2 2.6 collective-permute-start.9
  236.8 1.2 shard_map.53
  238.4 4.3 %all-to-all-done.1.got_ref = f32[8,128,256]{2,1,0:T(8,128)} async-done(((f32[8,128,256]{2,1,0:T(8,128)}), f32[8,128,256]{2,1,0:T(8,128)}, u32[]{:S(2)}, u32[]{:S(2)}) %all-to-all-start.1) | async-done | bytes 1048608 | tf_op jit(solution)/shard_map/all_to_all | solution.py:272
  242.7 1.7 shard_map.52
  244.5 71.6 %collective-permute-done.7 = f32[256,256]{1,0:T(8,128)} collective-permute-done((f32[256,256]{1,0:T(8,128)}, f32[256,256]{1,0:T(8,128)}, u32[]{:S(2)}, u32[]{:S(2)}) %collective-permute-start.7) | collective-permute-done | bytes 262176 | tf_op jit(solution)/shard_map/ppermute | solution.py:277
  318.3 3.5 %shard_map.56 = (f32[256,2048]{1,0:T(8,128)}, f32[256,128]{1,0:T(8,128)S(1)}, f32[256,128]{1,0:T(8,128)S(1)}) custom-call(f32[8,512]{1,0:T(8,128)S(1)} %slice_add_fusion.in_total_ref, f32[256,256]{1,0:T(8,128)S(1)} %add.154.refs_0_, f32[256,512]{1,0:T(8,128)S(1)} %add.155.refs_1_, f32[256,512]{1,0:T(8,128)S(1)} %get-tuple-element.66.refs_2_, ...), custom_call_target="tpu_custom_call" | custom-call | flops 9175040 | bytes 5505024 | tf_op jit(solution)/shard_map/pallas_call | solution.py:174
  322.6 1.7 collective-permute-start.10
  324.4 1.9 collective-permute-done.10
  (77 shorter events, 12.9 us)
Async XLA Ops:
  2.5 3.4 %copy-start = (f32[512,4096]{1,0:T(8,128)S(1)}, f32[512,4096]{1,0:T(8,128)}, u32[]{:S(2)}) copy-start(f32[512,4096]{1,0:T(8,128)} %x_ref.1) | copy-start | bytes 25165828
  5.9 11.5 %copy-start.15 = (s32[8192,1]{0,1:T(1,128)S(1)}, s32[8192,1]{0,1:T(1,128)}, u32[]{:S(2)}) copy-start(s32[8192,1]{0,1:T(1,128)} %param.3) | copy-start | bytes 98308
  12.1 3.2 copy-start.1
  15.4 14.3 %collective-permute-start = (f32[512,256]{1,0:T(8,128)S(1)}, f32[512,256]{1,0:T(8,128)S(1)}, u32[]{:S(2)}, u32[]{:S(2)}) collective-permute-start(f32[512,256]{1,0:T(8,128)S(1)} %get-tuple-element.39), channel_id=1, source_target_pairs={{0,1},{1,0},{2,3},{3,2},{4,5},{5,4},{6,7},{7,6},{8,9},{9,8},{10,11... | collective-permute-start | bytes 1572872 | tf_op jit(solution)/shard_map/ppermute | solution.py:263
  31.5 45.0 %all-to-all-start.2 = ((f32[8,128,256]{2,1,0:T(8,128)}), f32[8,128,256]{2,1,0:T(8,128)S(1)}, u32[]{:S(2)}, u32[]{:S(2)}) async-start(f32[8,128,256]{2,1,0:T(8,128)} %get-tuple-element.59), calls=%async_computation.2 | async-start | bytes 2097152 | tf_op jit(solution)/shard_map/all_to_all | solution.py:272
  36.1 3.4 %copy-start.2 = (bf16[1024,4096]{1,0:T(8,128)(2,1)S(1)}, bf16[1024,4096]{1,0:T(8,128)(2,1)}, u32[]{:S(2)}) copy-start(bf16[1024,4096]{1,0:T(8,128)(2,1)} %copy-done.1) | copy-start | bytes 25165828
  47.6 25.6 %collective-permute-start.1 = (f32[512,512]{1,0:T(8,128)S(1)}, f32[512,512]{1,0:T(8,128)S(1)}, u32[]{:S(2)}, u32[]{:S(2)}) collective-permute-start(f32[512,512]{1,0:T(8,128)S(1)} %get-tuple-element.43), channel_id=1, source_target_pairs={{0,1},{1,0},{2,3},{3,2},{4,5},{5,4},{6,7},{7,6},{8,9},{9,8},{10,11... | collective-permute-start | bytes 3145736 | tf_op jit(solution)/shard_map/ppermute | solution.py:263
  75.2 1.3 copy-start.9
  76.5 45.4 %all-to-all-start.3 = ((f32[8,128,512]{2,1,0:T(8,128)}), f32[8,128,512]{2,1,0:T(8,128)S(1)}, u32[]{:S(2)}, u32[]{:S(2)}) async-start(f32[8,128,512]{2,1,0:T(8,128)} %copy-done.9), calls=%async_computation.3 | async-start | bytes 4194304 | tf_op jit(solution)/shard_map/all_to_all | solution.py:272
  80.3 3.4 %copy-start.3 = (bf16[1024,4096]{1,0:T(8,128)(2,1)S(1)}, bf16[1024,4096]{1,0:T(8,128)(2,1)}, u32[]{:S(2)}) copy-start(bf16[1024,4096]{1,0:T(8,128)(2,1)} %copy-done.1) | copy-start | bytes 25165828
  91.3 27.2 %collective-permute-start.2 = (f32[512,512]{1,0:T(8,128)S(1)}, f32[512,512]{1,0:T(8,128)S(1)}, u32[]{:S(2)}, u32[]{:S(2)}) collective-permute-start(f32[512,512]{1,0:T(8,128)S(1)} %get-tuple-element.46), channel_id=1, source_target_pairs={{0,1},{1,0},{2,3},{3,2},{4,5},{5,4},{6,7},{7,6},{8,9},{9,8},{10,11... | collective-permute-start | bytes 3145736 | tf_op jit(solution)/shard_map/ppermute | solution.py:263
  120.5 1.3 copy-start.8
  121.9 1.3 copy-start.5
  123.2 62.6 %all-to-all-start.4 = ((f32[8,128,512]{2,1,0:T(8,128)}), f32[8,128,512]{2,1,0:T(8,128)}, u32[]{:S(2)}, u32[]{:S(2)}) async-start(f32[8,128,512]{2,1,0:T(8,128)} %copy-done.8), calls=%async_computation.4 | async-start | bytes 4194304 | tf_op jit(solution)/shard_map/all_to_all | solution.py:272
  127.6 3.4 %copy-start.4 = (bf16[1024,4096]{1,0:T(8,128)(2,1)S(1)}, bf16[1024,4096]{1,0:T(8,128)(2,1)}, u32[]{:S(2)}) copy-start(bf16[1024,4096]{1,0:T(8,128)(2,1)} %copy-done.1) | copy-start | bytes 25165828
  140.0 1.0 copy-start.13
  141.0 39.6 %collective-permute-start.4 = (f32[512,512]{1,0:T(8,128)}, f32[512,512]{1,0:T(8,128)S(1)}, u32[]{:S(2)}, u32[]{:S(2)}) collective-permute-start(f32[512,512]{1,0:T(8,128)} %get-tuple-element.52), channel_id=1, source_target_pairs={{0,1},{1,0},{2,3},{3,2},{4,5},{5,4},{6,7},{7,6},{8,9},{9,8},{10,11... | collective-permute-start | bytes 3145736 | tf_op jit(solution)/shard_map/ppermute | solution.py:263
  149.7 29.1 %collective-permute-start.3 = (f32[512,256]{1,0:T(8,128)S(1)}, f32[512,256]{1,0:T(8,128)S(1)}, u32[]{:S(2)}, u32[]{:S(2)}) collective-permute-start(f32[512,256]{1,0:T(8,128)S(1)} %get-tuple-element.49), channel_id=1, source_target_pairs={{0,1},{1,0},{2,3},{3,2},{4,5},{5,4},{6,7},{7,6},{8,9},{9,8},{10,11... | collective-permute-start | bytes 1572872 | tf_op jit(solution)/shard_map/ppermute | solution.py:263
  179.6 1.0 copy-start.10
  180.6 1.2 copy-start.14
  184.4 1.4 copy-start.7
  185.7 30.9 %all-to-all-start = ((f32[8,136,512]{2,1,0:T(8,128)}), f32[8,136,512]{2,1,0:T(8,128)S(1)}, u32[]{:S(2)}, u32[]{:S(2)}) async-start(f32[8,136,512]{2,1,0:T(8,128)} %copy-done.7), calls=%async_computation | async-start | bytes 4456448 | tf_op jit(solution)/shard_map/all_to_all | solution.py:272
  216.7 26.0 %all-to-all-start.1 = ((f32[8,128,256]{2,1,0:T(8,128)}), f32[8,128,256]{2,1,0:T(8,128)}, u32[]{:S(2)}, u32[]{:S(2)}) async-start(f32[8,128,256]{2,1,0:T(8,128)} %copy-done.10), calls=%async_computation.1 | async-start | bytes 2097152 | tf_op jit(solution)/shard_map/all_to_all | solution.py:272
  223.5 5.4 %copy-start.6 = (f32[8,128,512]{2,1,0:T(8,128)S(1)}, f32[8,128,512]{2,1,0:T(8,128)}, u32[]{:S(2)}) copy-start(f32[8,128,512]{2,1,0:T(8,128)} %copy-done.5) | copy-start | bytes 6291460
  225.5 0.8 copy-start.11
  226.3 91.9 %collective-permute-start.5 = (f32[264,512]{1,0:T(8,128)}, f32[264,512]{1,0:T(8,128)S(1)}, u32[]{:S(2)}, u32[]{:S(2)}) collective-permute-start(f32[264,512]{1,0:T(8,128)} %get-tuple-element.55), channel_id=1, source_target_pairs={{0,16},{2,18},{4,20},{6,22},{8,24},{10,26},{12,28},{14,30},{16,0},... | collective-permute-start | bytes 1622024 | tf_op jit(solution)/shard_map/ppermute | solution.py:277
  230.9 86.3 %collective-permute-start.8 = (f32[256,512]{1,0:T(8,128)}, f32[256,512]{1,0:T(8,128)}, u32[]{:S(2)}, u32[]{:S(2)}) collective-permute-start(f32[256,512]{1,0:T(8,128)} %get-tuple-element.64), channel_id=1, source_target_pairs={{0,16},{2,18},{4,20},{6,22},{8,24},{10,26},{12,28},{14,30},{16,0},... | collective-permute-start | bytes 1572872 | tf_op jit(solution)/shard_map/ppermute | solution.py:277
  234.2 84.0 %copy-start.12 = (f32[256,512]{1,0:T(8,128)S(1)}, f32[256,512]{1,0:T(8,128)}, u32[]{:S(2)}) copy-start(f32[256,512]{1,0:T(8,128)} %copy-done.11) | copy-start | bytes 1572868
  234.2 84.0 %collective-permute-start.9 = (f32[256,512]{1,0:T(8,128)}, f32[256,512]{1,0:T(8,128)}, u32[]{:S(2)}, u32[]{:S(2)}) collective-permute-start(f32[256,512]{1,0:T(8,128)} %get-tuple-element.67), channel_id=1, source_target_pairs={{0,16},{2,18},{4,20},{6,22},{8,24},{10,26},{12,28},{14,30},{16,0},... | collective-permute-start | bytes 1572872 | tf_op jit(solution)/shard_map/ppermute | solution.py:277
  238.1 78.1 %collective-permute-start.7 = (f32[256,256]{1,0:T(8,128)}, f32[256,256]{1,0:T(8,128)}, u32[]{:S(2)}, u32[]{:S(2)}) collective-permute-start(f32[256,256]{1,0:T(8,128)} %get-tuple-element.61), channel_id=1, source_target_pairs={{0,16},{2,18},{4,20},{6,22},{8,24},{10,26},{12,28},{14,30},{16,0},... | collective-permute-start | bytes 786440 | tf_op jit(solution)/shard_map/ppermute | solution.py:277
  244.5 77.4 %collective-permute-start.6 = (f32[256,256]{1,0:T(8,128)S(1)}, f32[256,256]{1,0:T(8,128)S(1)}, u32[]{:S(2)}, u32[]{:S(2)}) collective-permute-start(f32[256,256]{1,0:T(8,128)S(1)} %get-tuple-element.58), channel_id=1, source_target_pairs={{0,16},{2,18},{4,20},{6,22},{8,24},{10,26},{12,28},{14,30},{16,0},... | collective-permute-start | bytes 786440 | tf_op jit(solution)/shard_map/ppermute | solution.py:277
  322.6 3.7 %collective-permute-start.10 = (f32[8,256]{1,0:T(8,128)S(1)}, f32[8,256]{1,0:T(8,128)S(1)}, u32[]{:S(2)}, u32[]{:S(2)}) collective-permute-start(f32[8,256]{1,0:T(8,128)S(1)} %get-tuple-element.73), channel_id=1, source_target_pairs={{0,1},{1,0},{2,3},{3,2},{4,5},{5,4},{6,7},{7,6},{8,9},{9,8},{10,11... | collective-permute-start | bytes 24584 | tf_op jit(solution)/shard_map/ppermute | solution.py:289

commit v3 on v2

--- a/solution.py
+++ b/solution.py
@@ -40,12 +40,12 @@
     )
 
 
-def columns_kernel(start, owned, first, present_ref, pos_ref, x_ref, *refs):
+def columns_kernel(start, owned, first, targets, columns, present_ref, pos_ref, x_ref, *refs):
     sources = present_ref.shape[0]
     tile = x_ref.shape[1] // sources
     halves_ref, out_refs = (refs[0], refs[1:]) if first else (x_ref, refs)
     rows, width = out_refs[0].shape
-    per_column = present_ref.shape[1] // len(out_refs)
+    per_column = present_ref.shape[1] // columns
     for out_ref in out_refs:
         out_ref[...] = jnp.zeros_like(out_ref)
 
@@ -53,7 +53,7 @@
         at = pl.ds(pl.multiple_of(k * tile, tile), tile)
         if first:
             halves_ref[:rows, at], halves_ref[rows:, at] = split(x_ref[:, at])
-        for c, out_ref in enumerate(out_refs):
+        for c, out_ref in zip(targets, out_refs):
             for b in range(width // owned):
                 block = c * per_column + start // owned + b
 
@@ -67,16 +67,16 @@
     lax.fori_loop(0, sources, step, 0)
 
 
-def merge_columns(x, pos, present, owned, columns, start, width, first):
+def merge_columns(x, pos, present, owned, columns, start, width, first, targets):
     rows, cols = x.shape if first else (x.shape[0] // 2, x.shape[1])
     vmem = pl.BlockSpec(memory_space=pltpu.VMEM)
     halves = [jax.ShapeDtypeStruct((2 * rows, cols), BF16)] if first else []
     return call(
-        functools.partial(columns_kernel, start, owned, first),
-        2 * rows * cols * columns * width, 4 * rows * (cols + columns * width),
+        functools.partial(columns_kernel, start, owned, first, targets, columns),
+        2 * rows * cols * len(targets) * width, 4 * rows * (cols + len(targets) * width),
         in_specs=[pl.BlockSpec(memory_space=pltpu.SMEM), vmem, vmem],
-        out_specs=[vmem] * (len(halves) + columns),
-        out_shape=halves + [jax.ShapeDtypeStruct((rows, width), F32)] * columns,
+        out_specs=[vmem] * (len(halves) + len(targets)),
+        out_shape=halves + [jax.ShapeDtypeStruct((rows, width), F32)] * len(targets),
     )(present, pos, x)
 
 
@@ -122,29 +122,28 @@
     )(pos, *extra, *ins)
 
 
-def rows_kernel(pos_ref, got_ref, keep_ref, send_ref, *sum_refs):
-    peers, _, tile = got_ref.shape
-    owned, cap = keep_ref.shape[0], pos_ref.shape[1] // peers
-    for side, ref in enumerate((keep_ref, send_ref)):
+def rows_kernel(owned, pos_ref, got_ref, out_ref):
+    peers, depth, tile = got_ref.shape
+    cap = pos_ref.shape[1] // peers
+    for side in range(2):
         hi, lo = split(got_ref[:, side * cap : (side + 1) * cap].reshape(peers * cap, tile))
         table = hot(pos_ref[side : side + 1, :], owned)
-        ref[:owned] = mxu(table, hi, ((1,), (0,))) + mxu(table, lo, ((1,), (0,)))
-    for ref in sum_refs:
-        ref[...] = jnp.sum(got_ref[:, 2 * cap :], axis=0)
-        send_ref[owned:] = ref[...]
-
-
-def merge_rows(pos, got, owned, carrier):
+        out_ref[side * owned : (side + 1) * owned] = mxu(table, hi, ((1,), (0,))) + mxu(table, lo, ((1,), (0,)))
+    if depth > 2 * cap:
+        out_ref[2 * owned :] = jnp.sum(got_ref[:, 2 * cap :], axis=0)
+
+
+def merge_rows(pos, got, owned):
     peers, depth, width = got.shape
     slots = pos.shape[1]
+    height = 2 * owned + depth - 2 * slots // peers
     tile = min(width, 256)
-    heights = [owned, owned + 8, 8] if carrier else [owned, owned]
-    return call(
-        rows_kernel, 8 * owned * slots * width, 4 * width * (2 * owned + 2 * slots),
+    return call(
+        functools.partial(rows_kernel, owned), 8 * owned * slots * width, 4 * width * (2 * owned + 2 * slots),
         grid=(width // tile,),
         in_specs=[pl.BlockSpec((2, slots), lambda k: (0, 0)), pl.BlockSpec((peers, depth, tile), lambda k: (0, 0, k))],
-        out_specs=[pl.BlockSpec((h, tile), lambda k: (0, k)) for h in heights],
-        out_shape=[jax.ShapeDtypeStruct((h, width), F32) for h in heights],
+        out_specs=pl.BlockSpec((height, tile), lambda k: (0, k)),
+        out_shape=jax.ShapeDtypeStruct((height, width), F32),
     )(pos, got)
 
 
@@ -241,24 +240,36 @@
     owner = row_labels // owned
     table = (owner[:, None] == jnp.arange(groups, dtype=I32)[None, :]).astype(I32)
     rank = jnp.sum(jnp.cumsum(table, axis=0) * table, axis=1) - 1
-    place = lax.rem(owner, half) * 2 + (owner // half != blk // half).astype(I32)
+    side_of = blk // half
+    within = lax.rem(owner, half)
+    quarter = half // 2
+    inner = owner // half != side_of
+    aggregator = jnp.where(inner, 1 - side_of, side_of) * quarter + lax.rem(within, quarter)
+    place = aggregator * 2 + (within // quarter == side_of).astype(I32)
     row_pos = (place * cap + rank)[None, :]
 
     base = (blk // half) * half
     peers = lax.dynamic_slice_in_dim(ids.reshape(groups, rows), base, half, 0)
     take_pos = []
-    for agg in (blk, lax.rem(blk + half, groups)):
+    outer = lax.rem(blk, half) // quarter == side_of
+    served = jnp.where(outer, side_of, 1 - side_of) * half + lax.rem(blk, quarter)
+    for agg in (served + (1 - side_of) * quarter, served + side_of * quarter):
         tags = tags_of(peers, peers // owned == agg, cap).reshape(-1)
         take_pos.append(jnp.where(tags < 0, -1, tags - agg * owned))
     take_pos = jnp.stack(take_pos)
 
     n = len(plan)
     carrier = max(n - 2, 0)
-    keeps, others, halves, arrived = [], [], counts, []
+    keeps, others, halves, arrived = [], [], None, []
     for q, width in enumerate(plan):
-        parts = list(merge_columns(halves, col_pos[None, :], present, owned, columns, starts[q], width, q == 0))
+        merge = functools.partial(merge_columns, pos=col_pos[None, :], present=present, owned=owned, columns=columns)
+        if q:
+            parts = merge(halves, start=starts[q], width=width, first=False, targets=tuple(range(columns)))
+        else:
+            halves, *parts = merge(counts, start=0, width=width, first=True, targets=tuple(range(1, columns)))
         if q == 0:
-            halves = parts.pop(0)
+            parts = [*merge(halves, start=0, width=width, first=False, targets=(0,)), *parts]
+        parts = list(parts)
         for step in range(1, columns):
             parts[step] = lax.ppermute(parts[step], "col", [(i, (i + step) % columns) for i in range(columns)])
         arrived.append(parts)
@@ -273,11 +284,18 @@
             slotted[q], "blk", split_axis=0, concat_axis=0, tiled=True,
             axis_index_groups=[list(range(half)), list(range(half, groups))],
         )
-        keep, send, *half_sums = merge_rows(take_pos, got, owned, q == carrier)
-        others.append(lax.ppermute(send, "blk", [(i, (i + half) % groups) for i in range(groups)]))
+        both = merge_rows(take_pos, got, owned)
+        middle = [(quarter + r, half + r) for r in range(quarter)]
+        across = lax.ppermute(both, "blk", middle + [(j, i) for i, j in middle])
+        mine = jnp.where(outer, both[:2 * owned], across[:2 * owned])
+        send, keep = mine[:owned], mine[owned:]
+        if q == carrier:
+            send = jnp.concatenate([send, across[2 * owned :]], axis=0)
+        pairs = [(h * half + r, h * half + quarter + r) for h in range(2) for r in range(quarter)]
+        others.append(lax.ppermute(send, "blk", pairs + [(j, i) for i, j in pairs]))
         keeps.append(keep)
-        if half_sums:
-            in_total = half_sums[0] + others[q][owned:]
+        if q == carrier:
+            in_total = both[2 * owned :] + jnp.where(outer, others[q][owned:], across[2 * owned :])
     chunks = list(zip(keeps, others))
     for q in range(max(min(2, n - 3), 0)):
         chunks[q] = (keeps[q] + others[q],)

time: 328 us -> 338 us (1.030)
  starting transfers between devices: 38.4 us -> 117 us
  waiting for transfers between devices: 190 us -> 116 us
  local copies, waits for them, and re-layouts: 28.2 us -> 35.4 us
    ppermute x5 -> x10, starting transfers between devices: 5.92 us -> 84.8 us  [the longest x5 78.5 us: body(): others.append(lax.ppermute(send, 'blk', pairs + [(j, i) for i, j in pairs]))]
    ppermute x5 -> x10, waiting for transfers between devices: 71.6 us -> 22.6 us  [the longest x5 22.6 us: body(): others.append(lax.ppermute(send, 'blk', pairs + [(j, i) for i, j in pairs]))]
    all_to_all x5, waiting for transfers between devices: 28.7 us -> 1.45 us  [body(): lax.all_to_all(slotted[q], 'blk', split_axis=0, concat_axis=0, tiled=True...]
    unnamed x33 -> x39, local copies, waits for them, and re-layouts: 26.6 us -> 32.8 us
    pallas_call x10 -> x11, Pallas kernels: 46.9 us -> 45.1 us  [the longest x6 37.6 us: merge_columns(): call(functools.partial(columns_kernel, start, owned, first, targets, colu...]
  transfers between devices with their start and end apart: 16 -> 21, of which waited for: 8 -> 9; matrix products, arithmetic and copies ran while one was open for 3% -> 3% of each run, Pallas kernels for 16% -> 15%
where the time goes in v3:
time: 338 us; the launch traced here: 337 us
  starting transfers between devices  117 us (35%)
  waiting for transfers between devices  116 us (34%)
  Pallas kernels  57.5 us (17%)
  local copies, waits for them, and re-layouts  35.4 us (10%)
  other arithmetic  10.2 us (3%)
    ppermute x5, waiting for transfers between devices, body(): lax.ppermute(parts[step], 'col', [(i, (i + step) % columns) for i in rang...  90.1 us
    ppermute x5, starting transfers between devices, body(): others.append(lax.ppermute(send, 'blk', pairs + [(j, i) for i, j in pairs]))  78.5 us
    pallas_call x6, Pallas kernels, merge_columns(): call(functools.partial(columns_kernel, start, owned, first, targets, colu...  37.6 us
    unnamed x39, local copies, waits for them, and re-layouts  32.8 us
    ppermute x5, waiting for transfers between devices, body(): others.append(lax.ppermute(send, 'blk', pairs + [(j, i) for i, j in pairs]))  22.6 us
    all_to_all x5, starting transfers between devices, body(): lax.all_to_all(slotted[q], 'blk', split_axis=0, concat_axis=0, tiled=True...  20.3 us
    ppermute x5, starting transfers between devices, body(): lax.ppermute(parts[step], 'col', [(i, (i + step) % columns) for i in rang...  10.2 us
    pallas_call x5, Pallas kernels, fill_slots(): call(functools.partial(slots_kernel, carrier), 4 * slots * rows * width,...  9.83 us
  transfers between devices with their start and end apart: 21, of which 9 were waited for; matrix products, arithmetic and copies ran while one was open for 3% of the time, Pallas kernels for 15%

profile of v3, /device:TPU:0, one launch (start us, length us, event | category | flops | bytes accessed | tf_op | source)
XLA Modules:
  0.0 337.4 jit_solution(18339671623328857102)
XLA Ops:
  2.5 3.4 copy-done.6
  5.9 4.2 %shard_map.41 = (bf16[1024,4096]{1,0:T(8,128)(2,1)S(1)}, f32[512,256]{1,0:T(8,128)S(1)}) custom-call(s32[8,16]{1,0:T(8,128)S(1)} %convert_reduce_fusion.present_ref, s32[1,4096]{1,0:T(1,128)S(1)} %fusion.14.pos_ref, f32[512,4096]{1,0:T(8,128)S(1)} %copy-done.6), custom_call_target="tpu_custom_call" | custom-call | flops 1073741824 | bytes 8912896 | tf_op jit(solution)/shard_map/pallas_call | solution.py:74
  10.1 3.2 copy-done
  13.3 2.5 collective-permute-start
  17.4 3.4 %copy-done.1 = bf16[1024,4096]{1,0:T(8,128)(2,1)S(1)} copy-done((bf16[1024,4096]{1,0:T(8,128)(2,1)S(1)}, bf16[1024,4096]{1,0:T(8,128)(2,1)}, u32[]{:S(2)}) %copy-start.1) | copy-done | bytes 8388632
  20.8 2.7 shard_map.42.refs_0_
  23.5 4.2 %collective-permute-done.refs_1_ = f32[512,256]{1,0:T(8,128)S(1)} collective-permute-done((f32[512,256]{1,0:T(8,128)S(1)}, f32[512,256]{1,0:T(8,128)S(1)}, u32[]{:S(2)}, u32[]{:S(2)}) %collective-permute-start) | collective-permute-done | bytes 524320 | tf_op jit(solution)/shard_map/ppermute | solution.py:274
  27.8 1.7 shard_map.43
  29.4 4.5 %all-to-all-start.2 = ((f32[8,128,256]{2,1,0:T(8,128)}), f32[8,128,256]{2,1,0:T(8,128)S(1)}, u32[]{:S(2)}, u32[]{:S(2)}) async-start(f32[8,128,256]{2,1,0:T(8,128)} %get-tuple-element.42), calls=%async_computation.2 | async-start | bytes 2097152 | tf_op jit(solution)/shard_map/all_to_all | solution.py:283
  34.0 3.4 %copy-done.2 = bf16[1024,4096]{1,0:T(8,128)(2,1)S(1)} copy-done((bf16[1024,4096]{1,0:T(8,128)(2,1)S(1)}, bf16[1024,4096]{1,0:T(8,128)(2,1)}, u32[]{:S(2)}) %copy-start.2) | copy-done | bytes 8388632
  37.4 6.0 %shard_map.48 = (f32[512,256]{1,0:T(8,128)S(1)}, f32[512,256]{1,0:T(8,128)S(1)}) custom-call(s32[8,16]{1,0:T(8,128)S(1)} %convert_reduce_fusion.present_ref, s32[1,4096]{1,0:T(1,128)S(1)} %fusion.14.pos_ref, bf16[1024,4096]{1,0:T(8,128)(2,1)S(1)} %copy-done.2), custom_call_target="tpu_custom_call" | custom-call | flops 2147483648 | bytes 9437184 | tf_op jit(solution)/shard_map/pallas_call | solution.py:74
  43.4 14.3 %collective-permute-done.3.refs_1_ = f32[512,256]{1,0:T(8,128)S(1)} collective-permute-done((f32[512,256]{1,0:T(8,128)S(1)}, f32[512,256]{1,0:T(8,128)S(1)}, u32[]{:S(2)}, u32[]{:S(2)}) %collective-permute-start.3) | collective-permute-done | bytes 524320 | tf_op jit(solution)/shard_map/ppermute | solution.py:274
  57.7 1.7 shard_map.49
  59.4 3.8 %all-to-all-start.1 = ((f32[8,128,256]{2,1,0:T(8,128)}), f32[8,128,256]{2,1,0:T(8,128)S(1)}, u32[]{:S(2)}, u32[]{:S(2)}) async-start(f32[8,128,256]{2,1,0:T(8,128)} %get-tuple-element.41), calls=%async_computation.1 | async-start | bytes 2097152 | tf_op jit(solution)/shard_map/all_to_all | solution.py:283
  63.2 3.4 %copy-done.3 = bf16[1024,4096]{1,0:T(8,128)(2,1)S(1)} copy-done((bf16[1024,4096]{1,0:T(8,128)(2,1)S(1)}, bf16[1024,4096]{1,0:T(8,128)(2,1)}, u32[]{:S(2)}) %copy-start.3) | copy-done | bytes 8388632
  66.6 7.6 %shard_map.46 = (f32[512,512]{1,0:T(8,128)S(1)}, f32[512,512]{1,0:T(8,128)S(1)}) custom-call(s32[8,16]{1,0:T(8,128)S(1)} %convert_reduce_fusion.present_ref, s32[1,4096]{1,0:T(1,128)S(1)} %fusion.14.pos_ref, bf16[1024,4096]{1,0:T(8,128)(2,1)S(1)} %copy-done.3), custom_call_target="tpu_custom_call" | custom-call | flops 4294967296 | bytes 10485760 | tf_op jit(solution)/shard_map/pallas_call | solution.py:74
  74.3 2.2 collective-permute-start.2
  76.5 23.8 %collective-permute-done.2.refs_1_ = f32[512,512]{1,0:T(8,128)S(1)} collective-permute-done((f32[512,512]{1,0:T(8,128)S(1)}, f32[512,512]{1,0:T(8,128)S(1)}, u32[]{:S(2)}, u32[]{:S(2)}) %collective-permute-start.2) | collective-permute-done | bytes 1048608 | tf_op jit(solution)/shard_map/ppermute | solution.py:274
  100.3 2.0 shard_map.47
  104.7 3.8 %all-to-all-start.4 = ((f32[8,128,512]{2,1,0:T(8,128)}), f32[8,128,512]{2,1,0:T(8,128)S(1)}, u32[]{:S(2)}, u32[]{:S(2)}) async-start(f32[8,128,512]{2,1,0:T(8,128)} %copy-done.13), calls=%async_computation.4 | async-start | bytes 4194304 | tf_op jit(solution)/shard_map/all_to_all | solution.py:283
  108.5 3.4 %copy-done.4 = bf16[1024,4096]{1,0:T(8,128)(2,1)S(1)} copy-done((bf16[1024,4096]{1,0:T(8,128)(2,1)S(1)}, bf16[1024,4096]{1,0:T(8,128)(2,1)}, u32[]{:S(2)}) %copy-start.4) | copy-done | bytes 8388632
  111.9 8.1 %shard_map.44 = (f32[512,512]{1,0:T(8,128)S(1)}, f32[512,512]{1,0:T(8,128)S(1)}) custom-call(s32[8,16]{1,0:T(8,128)S(1)} %convert_reduce_fusion.present_ref, s32[1,4096]{1,0:T(1,128)S(1)} %fusion.14.pos_ref, bf16[1024,4096]{1,0:T(8,128)(2,1)S(1)} %copy-done.4), custom_call_target="tpu_custom_call" | custom-call | flops 4294967296 | bytes 10485760 | tf_op jit(solution)/shard_map/pallas_call | solution.py:74
  120.0 2.7 collective-permute-start.1
  122.7 23.8 %collective-permute-done.1.refs_1_ = f32[512,512]{1,0:T(8,128)S(1)} collective-permute-done((f32[512,512]{1,0:T(8,128)S(1)}, f32[512,512]{1,0:T(8,128)S(1)}, u32[]{:S(2)}, u32[]{:S(2)}) %collective-permute-start.1) | collective-permute-done | bytes 1048608 | tf_op jit(solution)/shard_map/ppermute | solution.py:274
  146.5 2.0 shard_map.45
  149.8 1.4 copy-done.7
  151.2 4.3 %all-to-all-start.3 = ((f32[8,128,512]{2,1,0:T(8,128)}), f32[8,128,512]{2,1,0:T(8,128)}, u32[]{:S(2)}, u32[]{:S(2)}) async-start(f32[8,128,512]{2,1,0:T(8,128)} %copy-done.12), calls=%async_computation.3 | async-start | bytes 4194304 | tf_op jit(solution)/shard_map/all_to_all | solution.py:283
  155.6 3.4 copy-done.5
  158.9 9.0 %shard_map.50 = (f32[512,512]{1,0:T(8,128)S(1)}, f32[512,512]{1,0:T(8,128)}) custom-call(s32[8,16]{1,0:T(8,128)S(1)} %convert_reduce_fusion.present_ref, s32[1,4096]{1,0:T(1,128)S(1)} %fusion.14.pos_ref, bf16[1024,4096]{1,0:T(8,128)(2,1)S(1)} %copy-done.5), custom_call_target="tpu_custom_call" | custom-call | flops 4294967296 | bytes 10485760 | tf_op jit(solution)/shard_map/pallas_call | solution.py:74
  168.9 2.7 collective-permute-start.4
  171.7 23.8 %collective-permute-done.4.refs_2_ = f32[512,512]{1,0:T(8,128)S(1)} collective-permute-done((f32[512,512]{1,0:T(8,128)}, f32[512,512]{1,0:T(8,128)S(1)}, u32[]{:S(2)}, u32[]{:S(2)}) %collective-permute-start.4) | collective-permute-done | bytes 1048608 | tf_op jit(solution)/shard_map/ppermute | solution.py:274
  196.8 2.5 shard_map.51
  200.7 3.8 %all-to-all-start = ((f32[8,136,512]{2,1,0:T(8,128)}), f32[8,136,512]{2,1,0:T(8,128)S(1)}, u32[]{:S(2)}, u32[]{:S(2)}) async-start(f32[8,136,512]{2,1,0:T(8,128)} %copy-done.11), calls=%async_computation | async-start | bytes 4456448 | tf_op jit(solution)/shard_map/all_to_all | solution.py:283
  211.0 2.4 shard_map.55
  213.4 1.6 collective-permute-start.11
  216.4 1.5 collective-permute-start.7
  217.8 2.0 shard_map.56
  219.9 1.7 collective-permute-start.13
  222.5 8.3 %collective-permute-start.10 = (f32[256,256]{1,0:T(8,128)}, f32[256,256]{1,0:T(8,128)S(1)}, u32[]{:S(2)}, u32[]{:S(2)}) collective-permute-start(f32[256,256]{1,0:T(8,128)} %slice.110), channel_id=1, source_target_pairs={{0,8},{2,10},{4,12},{6,14},{16,24},{18,26},{20,28},{22,30},{8,0},{... | collective-permute-start | bytes 786440 | tf_op jit(solution)/shard_map/ppermute | solution.py:295
  230.8 1.4 all-to-all-done.got_ref
  235.4 28.6 %collective-permute-start.8 = (f32[256,256]{1,0:T(8,128)S(1)}, f32[256,256]{1,0:T(8,128)S(1)}, u32[]{:S(2)}, u32[]{:S(2)}) collective-permute-start(f32[256,256]{1,0:T(8,128)S(1)} %get-tuple-element.61), channel_id=1, source_target_pairs={{0,8},{2,10},{4,12},{6,14},{16,24},{18,26},{20,28},{22,30},{8,0},{... | collective-permute-start | bytes 786440 | tf_op jit(solution)/shard_map/ppermute | solution.py:295
  265.6 1.4 broadcast_select_fusion
  267.5 40.1 %collective-permute-start.6 = (f32[264,512]{1,0:T(8,128)S(1)}, f32[264,512]{1,0:T(8,128)S(1)}, u32[]{:S(2)}, u32[]{:S(2)}) collective-permute-start(f32[264,512]{1,0:T(8,128)S(1)} %pad_maximum_fusion), channel_id=1, source_target_pairs={{0,8},{2,10},{4,12},{6,14},{16,24},{18,26},{20,28},{22,30},{8,0},{... | collective-permute-start | bytes 1622024 | tf_op jit(solution)/shard_map/ppermute | solution.py:295
  307.9 12.8 %collective-permute-done.6.refs_5_ = f32[264,512]{1,0:T(8,128)S(1)} collective-permute-done((f32[264,512]{1,0:T(8,128)S(1)}, f32[264,512]{1,0:T(8,128)S(1)}, u32[]{:S(2)}, u32[]{:S(2)}) %collective-permute-start.6) | collective-permute-done | bytes 540704 | tf_op jit(solution)/shard_map/ppermute | solution.py:295
  320.7 9.8 %collective-permute-done.14.refs_3_ = f32[256,512]{1,0:T(8,128)S(1)} collective-permute-done((f32[256,512]{1,0:T(8,128)S(1)}, f32[256,512]{1,0:T(8,128)S(1)}, u32[]{:S(2)}, u32[]{:S(2)}) %collective-permute-start.14) | collective-permute-done | bytes 524320 | tf_op jit(solution)/shard_map/ppermute | solution.py:295
  330.5 1.8 shard_map.57
  333.2 1.7 collective-permute-start.15
  334.9 1.9 collective-permute-done.15
  (106 shorter events, 26.3 us)
Async XLA Ops:
  2.5 3.4 %copy-start.6 = (f32[512,4096]{1,0:T(8,128)S(1)}, f32[512,4096]{1,0:T(8,128)}, u32[]{:S(2)}) copy-start(f32[512,4096]{1,0:T(8,128)} %x_ref.1) | copy-start | bytes 25165828
  5.9 9.9 %copy-start.18 = (s32[8192,1]{0,1:T(1,128)S(1)}, s32[8192,1]{0,1:T(1,128)}, u32[]{:S(2)}) copy-start(s32[8192,1]{0,1:T(1,128)} %param.3) | copy-start | bytes 98308
  10.1 3.2 copy-start
  13.3 14.4 %collective-permute-start = (f32[512,256]{1,0:T(8,128)S(1)}, f32[512,256]{1,0:T(8,128)S(1)}, u32[]{:S(2)}, u32[]{:S(2)}) collective-permute-start(f32[512,256]{1,0:T(8,128)S(1)} %get-tuple-element.27), channel_id=1, source_target_pairs={{0,1},{1,0},{2,3},{3,2},{4,5},{5,4},{6,7},{7,6},{8,9},{9,8},{10,11... | collective-permute-start | bytes 1572872 | tf_op jit(solution)/shard_map/ppermute | solution.py:274
  17.4 3.4 %copy-start.1 = (bf16[1024,4096]{1,0:T(8,128)(2,1)S(1)}, bf16[1024,4096]{1,0:T(8,128)(2,1)}, u32[]{:S(2)}) copy-start(bf16[1024,4096]{1,0:T(8,128)(2,1)} %copy-done) | copy-start | bytes 25165828
  29.4 30.0 %all-to-all-start.2 = ((f32[8,128,256]{2,1,0:T(8,128)}), f32[8,128,256]{2,1,0:T(8,128)S(1)}, u32[]{:S(2)}, u32[]{:S(2)}) async-start(f32[8,128,256]{2,1,0:T(8,128)} %get-tuple-element.42), calls=%async_computation.2 | async-start | bytes 2097152 | tf_op jit(solution)/shard_map/all_to_all | solution.py:283
  34.0 3.4 %copy-start.2 = (bf16[1024,4096]{1,0:T(8,128)(2,1)S(1)}, bf16[1024,4096]{1,0:T(8,128)(2,1)}, u32[]{:S(2)}) copy-start(bf16[1024,4096]{1,0:T(8,128)(2,1)} %copy-done) | copy-start | bytes 25165828
  43.3 14.4 %collective-permute-start.3 = (f32[512,256]{1,0:T(8,128)S(1)}, f32[512,256]{1,0:T(8,128)S(1)}, u32[]{:S(2)}, u32[]{:S(2)}) collective-permute-start(f32[512,256]{1,0:T(8,128)S(1)} %get-tuple-element.36), channel_id=1, source_target_pairs={{0,1},{1,0},{2,3},{3,2},{4,5},{5,4},{6,7},{7,6},{8,9},{9,8},{10,11... | collective-permute-start | bytes 1572872 | tf_op jit(solution)/shard_map/ppermute | solution.py:274
  59.4 44.2 %all-to-all-start.1 = ((f32[8,128,256]{2,1,0:T(8,128)}), f32[8,128,256]{2,1,0:T(8,128)S(1)}, u32[]{:S(2)}, u32[]{:S(2)}) async-start(f32[8,128,256]{2,1,0:T(8,128)} %get-tuple-element.41), calls=%async_computation.1 | async-start | bytes 2097152 | tf_op jit(solution)/shard_map/all_to_all | solution.py:283
  63.2 3.4 %copy-start.3 = (bf16[1024,4096]{1,0:T(8,128)(2,1)S(1)}, bf16[1024,4096]{1,0:T(8,128)(2,1)}, u32[]{:S(2)}) copy-start(bf16[1024,4096]{1,0:T(8,128)(2,1)} %copy-done) | copy-start | bytes 25165828
  74.3 26.0 %collective-permute-start.2 = (f32[512,512]{1,0:T(8,128)S(1)}, f32[512,512]{1,0:T(8,128)S(1)}, u32[]{:S(2)}, u32[]{:S(2)}) collective-permute-start(f32[512,512]{1,0:T(8,128)S(1)} %get-tuple-element.33), channel_id=1, source_target_pairs={{0,1},{1,0},{2,3},{3,2},{4,5},{5,4},{6,7},{7,6},{8,9},{9,8},{10,11... | collective-permute-start | bytes 3145736 | tf_op jit(solution)/shard_map/ppermute | solution.py:274
  102.3 1.4 copy-start.13
  103.7 1.0 copy-start.9
  104.7 45.1 %all-to-all-start.4 = ((f32[8,128,512]{2,1,0:T(8,128)}), f32[8,128,512]{2,1,0:T(8,128)S(1)}, u32[]{:S(2)}, u32[]{:S(2)}) async-start(f32[8,128,512]{2,1,0:T(8,128)} %copy-done.13), calls=%async_computation.4 | async-start | bytes 4194304 | tf_op jit(solution)/shard_map/all_to_all | solution.py:283
  108.5 3.4 %copy-start.4 = (bf16[1024,4096]{1,0:T(8,128)(2,1)S(1)}, bf16[1024,4096]{1,0:T(8,128)(2,1)}, u32[]{:S(2)}) copy-start(bf16[1024,4096]{1,0:T(8,128)(2,1)} %copy-done) | copy-start | bytes 25165828
  120.0 26.6 %collective-permute-start.1 = (f32[512,512]{1,0:T(8,128)S(1)}, f32[512,512]{1,0:T(8,128)S(1)}, u32[]{:S(2)}, u32[]{:S(2)}) collective-permute-start(f32[512,512]{1,0:T(8,128)S(1)} %get-tuple-element.30), channel_id=1, source_target_pairs={{0,1},{1,0},{2,3},{3,2},{4,5},{5,4},{6,7},{7,6},{8,9},{9,8},{10,11... | collective-permute-start | bytes 3145736 | tf_op jit(solution)/shard_map/ppermute | solution.py:274
  148.5 1.3 copy-start.12
  149.8 1.4 copy-start.7
  151.2 49.5 %all-to-all-start.3 = ((f32[8,128,512]{2,1,0:T(8,128)}), f32[8,128,512]{2,1,0:T(8,128)}, u32[]{:S(2)}, u32[]{:S(2)}) async-start(f32[8,128,512]{2,1,0:T(8,128)} %copy-done.12), calls=%async_computation.3 | async-start | bytes 4194304 | tf_op jit(solution)/shard_map/all_to_all | solution.py:283
  155.5 3.4 %copy-start.5 = (bf16[1024,4096]{1,0:T(8,128)(2,1)S(1)}, bf16[1024,4096]{1,0:T(8,128)(2,1)}, u32[]{:S(2)}) copy-start(bf16[1024,4096]{1,0:T(8,128)(2,1)} %copy-done) | copy-start | bytes 25165828
  168.0 1.0 copy-start.14
  168.9 26.6 %collective-permute-start.4 = (f32[512,512]{1,0:T(8,128)}, f32[512,512]{1,0:T(8,128)S(1)}, u32[]{:S(2)}, u32[]{:S(2)}) collective-permute-start(f32[512,512]{1,0:T(8,128)} %get-tuple-element.39), channel_id=1, source_target_pairs={{0,1},{1,0},{2,3},{3,2},{4,5},{5,4},{6,7},{7,6},{8,9},{9,8},{10,11... | collective-permute-start | bytes 3145736 | tf_op jit(solution)/shard_map/ppermute | solution.py:274
  195.6 1.2 copy-start.15
  199.3 1.4 copy-start.11
  200.7 31.5 %all-to-all-start = ((f32[8,136,512]{2,1,0:T(8,128)}), f32[8,136,512]{2,1,0:T(8,128)S(1)}, u32[]{:S(2)}, u32[]{:S(2)}) async-start(f32[8,136,512]{2,1,0:T(8,128)} %copy-done.11), calls=%async_computation | async-start | bytes 4456448 | tf_op jit(solution)/shard_map/all_to_all | solution.py:283
  209.7 5.4 %copy-start.10 = (f32[8,128,256]{2,1,0:T(8,128)S(1)}, f32[8,128,256]{2,1,0:T(8,128)}, u32[]{:S(2)}) copy-start(f32[8,128,256]{2,1,0:T(8,128)} %copy-done.9) | copy-start | bytes 3145732
  210.2 7.6 %copy-start.8 = (f32[8,128,512]{2,1,0:T(8,128)S(1)}, f32[8,128,512]{2,1,0:T(8,128)}, u32[]{:S(2)}) copy-start(f32[8,128,512]{2,1,0:T(8,128)} %copy-done.7) | copy-start | bytes 6291460
  210.2 11.3 %collective-permute-start.9 = (f32[512,256]{1,0:T(8,128)S(1)}, f32[512,256]{1,0:T(8,128)S(1)}, u32[]{:S(2)}, u32[]{:S(2)}) collective-permute-start(f32[512,256]{1,0:T(8,128)S(1)} %shard_map.54), channel_id=1, source_target_pairs={{8,16},{10,18},{12,20},{14,22},{16,8},{18,10},{20,12},{22,14},{9,1... | collective-permute-start | bytes 1572872 | tf_op jit(solution)/shard_map/ppermute | solution.py:289
  213.4 50.6 %collective-permute-start.11 = (f32[512,512]{1,0:T(8,128)S(1)}, f32[512,512]{1,0:T(8,128)}, u32[]{:S(2)}, u32[]{:S(2)}) collective-permute-start(f32[512,512]{1,0:T(8,128)S(1)} %shard_map.55), channel_id=1, source_target_pairs={{8,16},{10,18},{12,20},{14,22},{16,8},{18,10},{20,12},{22,14},{9,1... | collective-permute-start | bytes 3145736 | tf_op jit(solution)/shard_map/ppermute | solution.py:289
  216.4 17.9 %collective-permute-start.7 = (f32[512,256]{1,0:T(8,128)}, f32[512,256]{1,0:T(8,128)}, u32[]{:S(2)}, u32[]{:S(2)}) collective-permute-start(f32[512,256]{1,0:T(8,128)} %shard_map.53), channel_id=1, source_target_pairs={{8,16},{10,18},{12,20},{14,22},{16,8},{18,10},{20,12},{22,14},{9,1... | collective-permute-start | bytes 1572872 | tf_op jit(solution)/shard_map/ppermute | solution.py:289
  219.9 45.8 %collective-permute-start.13 = (f32[512,512]{1,0:T(8,128)}, f32[512,512]{1,0:T(8,128)}, u32[]{:S(2)}, u32[]{:S(2)}) collective-permute-start(f32[512,512]{1,0:T(8,128)} %shard_map.56), channel_id=1, source_target_pairs={{8,16},{10,18},{12,20},{14,22},{16,8},{18,10},{20,12},{22,14},{9,1... | collective-permute-start | bytes 3145736 | tf_op jit(solution)/shard_map/ppermute | solution.py:289
  221.6 0.9 copy-start.16
  222.5 85.3 %collective-permute-start.10 = (f32[256,256]{1,0:T(8,128)}, f32[256,256]{1,0:T(8,128)S(1)}, u32[]{:S(2)}, u32[]{:S(2)}) collective-permute-start(f32[256,256]{1,0:T(8,128)} %slice.110), channel_id=1, source_target_pairs={{0,8},{2,10},{4,12},{6,14},{16,24},{18,26},{20,28},{22,30},{8,0},{... | collective-permute-start | bytes 786440 | tf_op jit(solution)/shard_map/ppermute | solution.py:295
  233.5 33.6 %collective-permute-start.5 = (f32[520,512]{1,0:T(8,128)S(1)}, f32[520,512]{1,0:T(8,128)S(1)}, u32[]{:S(2)}, u32[]{:S(2)}) collective-permute-start(f32[520,512]{1,0:T(8,128)S(1)} %shard_map.52), channel_id=1, source_target_pairs={{8,16},{10,18},{12,20},{14,22},{16,8},{18,10},{20,12},{22,14},{9,1... | collective-permute-start | bytes 3194888 | tf_op jit(solution)/shard_map/ppermute | solution.py:289
  235.4 97.0 %collective-permute-start.8 = (f32[256,256]{1,0:T(8,128)S(1)}, f32[256,256]{1,0:T(8,128)S(1)}, u32[]{:S(2)}, u32[]{:S(2)}) collective-permute-start(f32[256,256]{1,0:T(8,128)S(1)} %get-tuple-element.61), channel_id=1, source_target_pairs={{0,8},{2,10},{4,12},{6,14},{16,24},{18,26},{20,28},{22,30},{8,0},{... | collective-permute-start | bytes 786440 | tf_op jit(solution)/shard_map/ppermute | solution.py:295
  264.3 43.5 %collective-permute-start.12 = (f32[256,512]{1,0:T(8,128)S(1)}, f32[256,512]{1,0:T(8,128)S(1)}, u32[]{:S(2)}, u32[]{:S(2)}) collective-permute-start(f32[256,512]{1,0:T(8,128)S(1)} %slice.112), channel_id=1, source_target_pairs={{0,8},{2,10},{4,12},{6,14},{16,24},{18,26},{20,28},{22,30},{8,0},{... | collective-permute-start | bytes 1572872 | tf_op jit(solution)/shard_map/ppermute | solution.py:295
  267.4 40.4 %copy-start.17 = (f32[512,256]{1,0:T(8,128)S(1)}, f32[512,256]{1,0:T(8,128)}, u32[]{:S(2)}) copy-start(f32[512,256]{1,0:T(8,128)} %copy-done.16) | copy-start | bytes 1572868
  267.5 53.3 %collective-permute-start.6 = (f32[264,512]{1,0:T(8,128)S(1)}, f32[264,512]{1,0:T(8,128)S(1)}, u32[]{:S(2)}, u32[]{:S(2)}) collective-permute-start(f32[264,512]{1,0:T(8,128)S(1)} %pad_maximum_fusion), channel_id=1, source_target_pairs={{0,8},{2,10},{4,12},{6,14},{16,24},{18,26},{20,28},{22,30},{8,0},{... | collective-permute-start | bytes 1622024 | tf_op jit(solution)/shard_map/ppermute | solution.py:295
  307.7 22.9 %collective-permute-start.14 = (f32[256,512]{1,0:T(8,128)S(1)}, f32[256,512]{1,0:T(8,128)S(1)}, u32[]{:S(2)}, u32[]{:S(2)}) collective-permute-start(f32[256,512]{1,0:T(8,128)S(1)} %get-tuple-element.59), channel_id=1, source_target_pairs={{0,8},{2,10},{4,12},{6,14},{16,24},{18,26},{20,28},{22,30},{8,0},{... | collective-permute-start | bytes 1572872 | tf_op jit(solution)/shard_map/ppermute | solution.py:295
  333.2 3.7 %collective-permute-start.15 = (f32[8,256]{1,0:T(8,128)S(1)}, f32[8,256]{1,0:T(8,128)S(1)}, u32[]{:S(2)}, u32[]{:S(2)}) collective-permute-start(f32[8,256]{1,0:T(8,128)S(1)} %get-tuple-element.49), channel_id=1, source_target_pairs={{0,1},{1,0},{2,3},{3,2},{4,5},{5,4},{6,7},{7,6},{8,9},{9,8},{10,11... | collective-permute-start | bytes 24584 | tf_op jit(solution)/shard_map/ppermute | solution.py:307
